TPU v7x, 32 devices: a whole 2x2x4 slice. The times are simulated.
32 devices in a mesh: row: 8 (over z, x), col: 4 (over y, core).
Axes of the slice: x: 2, y: 2, z: 4, core: 2. Of those that a mesh axis runs over, the one named last changes fastest.
Arguments:
- matrix: float32 [5, 8, 10, 4, 128, 128], P(None, 'row', None, 'col'), may hold values from 0 to 2.5, as said below
- flags: int32 [5, 8, 10, 4], P(None, 'row', None, 'col'), may hold values from 0 to 1, as said below
Outputs:
- factor: float32 [5, 8, 10, 4, 128, 128], P(None, 'row', None, 'col')
Inputs may be any that keep to these rules, and one draw needn't show every extreme that they name: `matrix`: symmetric positive definite, of order 40*128, diagonal at least 1.5. `flags`: 0 marks a float32 tile, 1 a bfloat16 tile; every diagonal tile is 0.
All inputs are finite; a program needn't handle non-finite values.
Results may differ from a plain program's by a relative error of at most 0.0005.
The roundings to bfloat16 on the way count: a program that leaves them out, or rounds other values in their place, can miss the bound.
Values sent between devices are 32-bit elements; how exact they have to be, the bound alone decides.
A program may use at most 128 MiB of HBM per device.

v0:
```python
import jax
import jax.numpy as jnp
from jax import lax
from jax.experimental import pallas as pl
from jax.experimental.pallas import tpu as pltpu
from jax.sharding import PartitionSpec as P

PT = 4
MICRO = 16
NT_DIMS = (((1,), (1,)), ((), ()))
TN_DIMS = (((0,), (0,)), ((), ()))


def dot_nt(a, b):
    return lax.dot_general(
        a, b, NT_DIMS, precision=lax.Precision.HIGHEST, preferred_element_type=jnp.float32
    )


def dot_nt_coarse(a, b):
    return lax.dot_general(
        a.astype(jnp.bfloat16),
        b.astype(jnp.bfloat16),
        NT_DIMS,
        preferred_element_type=jnp.float32,
    )


def split(value):
    high = value.astype(jnp.bfloat16)
    return high, (value - high.astype(jnp.float32)).astype(jnp.bfloat16)


def dot_bf16(a, b):
    return lax.dot_general(a, b, NT_DIMS, preferred_element_type=jnp.float32)


def dot_pairs(a, b):
    return dot_bf16(a[0], b[0]) + (dot_bf16(a[0], b[1]) + dot_bf16(a[1], b[0]))


def factor_tile(start, work_ref, low_ref, inv_ref):
    tile = start.shape[0]
    lane = lax.broadcasted_iota(jnp.int32, (tile, tile), 1)
    sub = lax.broadcasted_iota(jnp.int32, (tile, tile), 0)
    work_ref[:, :tile] = start
    work_ref[:, tile:] = (lane == sub).astype(jnp.float32)
    lane8 = lax.broadcasted_iota(jnp.int32, (MICRO, tile), 1)
    sub8 = lax.broadcasted_iota(jnp.int32, (MICRO, tile), 0)

    def micro(p, carry):
        base = pl.multiple_of(p * MICRO, MICRO)
        both = work_ref[pl.ds(base, MICRO), :]
        turned = pltpu.roll(both[:, :tile], lax.rem(tile - base, tile), 1)
        s = {}
        for k in range(MICRO):
            for q in range(k + 1):
                s[k, q] = jnp.broadcast_to(turned[k : k + 1, q : q + 1], (1, tile))
        rows = [both[k : k + 1, :tile] for k in range(MICRO)]
        more = [both[k : k + 1, tile:] for k in range(MICRO)]
        for q in range(MICRO):
            d = s[q, q]
            r = lax.rsqrt(d)
            r = r * (1.5 - 0.5 * d * r * r)
            rows[q] = rows[q] * r
            more[q] = more[q] * r
            low = {k: s[k, q] * r for k in range(q + 1, MICRO)}
            for k in range(q + 1, MICRO):
                for m in range(q + 1, k + 1):
                    s[k, m] = s[k, m] - low[k] * low[m]
                rows[k] = rows[k] - low[k] * rows[q]
                more[k] = more[k] - low[k] * more[q]
        upper = jnp.where(lane8 >= base + sub8, jnp.concatenate(rows, axis=0), 0.0)
        extra = jnp.concatenate(more, axis=0)
        low_ref[pl.ds(base, MICRO), :] = upper
        inv_ref[pl.ds(base, MICRO), :] = extra
        work_ref[...] -= lax.dot_general(
            upper,
            jnp.concatenate([upper, extra], axis=1),
            TN_DIMS,
            precision=lax.Precision.HIGHEST,
            preferred_element_type=jnp.float32,
        )
        return carry

    lax.fori_loop(0, tile // MICRO, micro, 0)


def factor_kernel(step, col_count, tile, grid_ref, *refs):
    if step:
        before_ref, low_ref, inv_ref, work_ref, up_ref = refs
    else:
        low_ref, inv_ref, work_ref, up_ref = refs
    first = step * PT
    count = 2 * PT - first
    lane = lax.broadcasted_iota(jnp.int32, (tile, tile), 1)
    sub = lax.broadcasted_iota(jnp.int32, (tile, tile), 0)

    def span(i, j=None):
        return slice(i * tile, (i + 1 if j is None else j) * tile)

    for i in range(count):
        for j in range(PT):
            if j > i:
                low_ref[span(i), span(j)] = jnp.zeros((tile, tile), jnp.float32)
                continue
            where = (first + i, (first + j) % col_count, (first + j) // col_count)
            piece = grid_ref[(*where, slice(0, tile))]
            if i == j:
                kept = jnp.where(lane <= sub, piece, 0.0)
                piece = kept + jnp.where(lane < sub, piece, 0.0).T
            if step:
                left = before_ref[span(PT + i), :]
                right = before_ref[span(PT + j), :]
                mark = grid_ref[(*where, slice(tile, tile + 1))]
                piece = piece - jnp.where(mark > 0.5, dot_nt_coarse(left, right), dot_nt(left, right))
            low_ref[span(i), span(j)] = piece
    for t in range(PT):
        factor_tile(low_ref[span(t), span(t)], work_ref, up_ref, inv_ref.at[t])
        low_ref[span(t), span(t)] = up_ref[...].T
        if t + 1 < count:
            solved = dot_nt(low_ref[span(t + 1, count), span(t)], inv_ref[t])
            low_ref[span(t + 1, count), span(t)] = solved
            for u in range(t + 1, PT):
                low_ref[span(u, count), span(u)] -= dot_nt(
                    low_ref[span(u, count), span(t)], low_ref[span(u), span(t)]
                )


def factor_blocks(step, grid, *before):
    col_count = grid.shape[1]
    tile = grid.shape[4]
    count = 2 * PT - step * PT
    vmem = pl.BlockSpec(memory_space=pltpu.VMEM)
    return pl.pallas_call(
        lambda *refs: factor_kernel(step, col_count, tile, *refs),
        out_shape=(
            jax.ShapeDtypeStruct((count * tile, PT * tile), jnp.float32),
            jax.ShapeDtypeStruct((PT, tile, tile), jnp.float32),
        ),
        in_specs=[vmem] * (1 + len(before)),
        out_specs=(vmem, vmem),
        scratch_shapes=[
            pltpu.VMEM((tile, 2 * tile), jnp.float32),
            pltpu.VMEM((tile, tile), jnp.float32),
        ],
        cost_estimate=pl.CostEstimate(flops=20_000_000_000, bytes_accessed=9_000_000, transcendentals=0),
        name="factor_blocks",
    )(grid, *before)


def solve_kernel(tile, groups, ids_ref, order_ref, panel_ref, low0_ref, inv0_ref, low1_ref, inv1_ref,
                 high_ref, rest_ref, low_h, low_l, inv_h, inv_l):
    count = 2 * PT
    width = PT * tile
    rows = panel_ref.shape[1]
    col_count = panel_ref.shape[0]
    group = pl.program_id(0)

    def span(i, j=None):
        return slice(i * tile, (i + 1 if j is None else j) * tile)

    @pl.when(group == 0)
    def _():
        for i in range(count):
            low_h[span(i), :width], low_l[span(i), :width] = split(low0_ref[span(i), :])
        for i in range(PT):
            at = PT + i
            low_h[span(at), width:], low_l[span(at), width:] = split(low1_ref[span(i), :])
            low_h[span(i), width:] = jnp.zeros((tile, width), jnp.bfloat16)
            low_l[span(i), width:] = jnp.zeros((tile, width), jnp.bfloat16)
            inv_h[i], inv_l[i] = split(inv0_ref[i])
            inv_h[at], inv_l[at] = split(inv1_ref[i])

    def flat(value):
        return value.reshape(rows * tile, tile)

    for t in range(count):
        first = t // PT * PT
        slot = t // col_count
        owner = order_ref[t]
        value = flat(panel_ref[owner, :, slot, :tile, :])
        if first:
            left = (high_ref[0, :, :width], rest_ref[0, :, :width])
            right = (low_h[span(t), :width], low_l[span(t), :width])
            coarse = dot_bf16(left[0], right[0])
            exact = coarse + (dot_bf16(left[0], right[1]) + dot_bf16(left[1], right[0]))
            mark = panel_ref[owner, :, slot, tile : tile + 1, :]
            mark = flat(jnp.broadcast_to(mark, (rows, tile, tile)))
            value = value - jnp.where(mark > 0.5, coarse, exact)
        if t > first:
            value = value - dot_pairs(
                (high_ref[0, :, span(first, t)], rest_ref[0, :, span(first, t)]),
                (low_h[span(t), span(first, t)], low_l[span(t), span(first, t)]),
            )
        high_ref[0, :, span(t)], rest_ref[0, :, span(t)] = split(
            dot_pairs(split(value), (inv_h[t], inv_l[t]))
        )

    row = ids_ref[group]

    @pl.when(row < count)
    def _():
        base = pl.multiple_of(jnp.minimum(row, count - 1) * tile, tile)
        high_ref[0, :tile, :] = low_h[pl.ds(base, tile), :]
        rest_ref[0, :tile, :] = low_l[pl.ds(base, tile), :]


def solve_panels(ids, order, panels, factors, groups):
    col_count = panels.shape[0] // groups
    _, rows, slots, height, tile = panels.shape
    count = 2 * PT
    full = count * tile
    keep = lambda n: (lambda g, *refs: (0,) * n)
    out_spec = pl.BlockSpec((1, rows * tile, full), lambda g, *refs: (g, 0, 0))
    out_shape = jax.ShapeDtypeStruct((groups, rows * tile, full), jnp.bfloat16)
    return pl.pallas_call(
        lambda *refs: solve_kernel(tile, groups, *refs),
        grid_spec=pltpu.PrefetchScalarGridSpec(
            num_scalar_prefetch=2,
            grid=(groups,),
            in_specs=[
                pl.BlockSpec((col_count, rows, slots, height, tile), lambda g, *refs: (g, 0, 0, 0, 0))
            ]
            + [pl.BlockSpec(f.shape, keep(len(f.shape))) for f in factors],
            out_specs=(out_spec, out_spec),
            scratch_shapes=[
                pltpu.VMEM((full, full), jnp.bfloat16),
                pltpu.VMEM((full, full), jnp.bfloat16),
                pltpu.VMEM((count, tile, tile), jnp.bfloat16),
                pltpu.VMEM((count, tile, tile), jnp.bfloat16),
            ],
        ),
        out_shape=(out_shape, out_shape),
        compiler_params=pltpu.CompilerParams(vmem_limit_bytes=56 * 1024 * 1024),
        cost_estimate=pl.CostEstimate(
            flops=groups * 4_000_000_000, bytes_accessed=groups * 6_000_000, transcendentals=0
        ),
        name="solve_panels",
    )(ids, order, panels, *factors)


def update_kernel(tile, groups, rows_ref, cols_ref, marks_ref, raw_ref, left_h, left_l, right_h, right_l, out_ref):
    count = 2 * PT
    b = pl.program_id(0)
    j = cols_ref[b]
    base = pl.multiple_of(jnp.minimum(j, count - 1) * tile, tile)
    at = pl.multiple_of(b // groups * tile, tile)
    group = b % groups

    def rounded(value):
        return value.astype(jnp.bfloat16).astype(jnp.float32)

    def tile_row(a):
        i = rows_ref[a]
        mark = marks_ref[a * pl.num_programs(0) + b]
        mine = slice(a * tile, (a + 1) * tile)

        @pl.when(i < j)
        def _():
            out_ref[a, 0] = jnp.zeros((tile, tile), jnp.float32)

        @pl.when((i >= j) & (j < count))
        def _():
            high = left_h[0, mine, pl.ds(base, tile)].astype(jnp.float32)
            rest = left_l[0, mine, pl.ds(base, tile)].astype(jnp.float32)
            out_ref[a, 0] = high + jnp.where(mark == 1, 0.0, rest)

        @pl.when((i >= j) & (j >= count) & (mark == 1))
        def _():
            other = right_h[group, pl.ds(at, tile), :]
            out_ref[a, 0] = rounded(rounded(raw_ref[a, 0]) - dot_bf16(left_h[0, mine, :], other))

        @pl.when((i >= j) & (j >= count) & (mark != 1))
        def _():
            high = right_h[group, pl.ds(at, tile), :]
            rest = right_l[group, pl.ds(at, tile), :]
            out_ref[a, 0] = raw_ref[a, 0] - dot_pairs(
                (left_h[0, mine, :], left_l[0, mine, :]), (high, rest)
            )

    for a in range(raw_ref.shape[0]):
        tile_row(a)


def update_tiles(row_ids, col_ids, marks, tiles, left, right):
    rows, cols, tile, _ = tiles.shape
    groups = right[0].shape[0]
    whole = lambda b, *refs: (0, 0, 0)
    each = pl.BlockSpec((rows, 1, tile, tile), lambda b, *refs: (0, b, 0, 0))
    return pl.pallas_call(
        lambda *refs: update_kernel(tile, groups, *refs),
        grid_spec=pltpu.PrefetchScalarGridSpec(
            num_scalar_prefetch=3,
            grid=(cols,),
            in_specs=[each] + [pl.BlockSpec(v.shape, whole) for v in (*left, *right)],
            out_specs=each,
        ),
        out_shape=jax.ShapeDtypeStruct(tiles.shape, jnp.float32),
        compiler_params=pltpu.CompilerParams(vmem_limit_bytes=60 * 1024 * 1024),
        name="update_tiles",
    )(row_ids, col_ids, marks.reshape(-1), tiles, *left, *right)


def on_device(matrix, flags):
    row_count = lax.axis_size("row")
    col_count = lax.axis_size("col")
    row_index = lax.axis_index("row")
    col_index = lax.axis_index("col")
    tile_rows = matrix.shape[0]
    tile_cols = matrix.shape[2]
    tile = matrix.shape[4]
    count = 2 * PT
    slots = count // col_count
    groups = row_count // col_count
    tiles = matrix.reshape(tile_rows, tile_cols, tile, tile)
    marks = flags.reshape(tile_rows, tile_cols)
    row_ids = jnp.arange(tile_rows, dtype=jnp.int32) * row_count + row_index
    col_ids = jnp.arange(tile_cols, dtype=jnp.int32) * col_count + col_index

    head = tiles[:, :slots]
    head_marks = (marks[:, :slots] == 1)[:, :, None, None]
    stored = jnp.where(head_marks, lax.reduce_precision(head, 8, 7), head)
    tags = jnp.broadcast_to(head_marks.astype(jnp.float32), (tile_rows, slots, 8, tile))
    payload = jnp.concatenate([stored, tags], axis=2)

    grid = lax.all_gather(payload[0], ("row", "col"))
    grid = grid.reshape(row_count, col_count, slots, tile + 8, tile)[:count]
    low0, inv0 = factor_blocks(0, grid)
    low1, inv1 = factor_blocks(1, grid, low0)
    factors = (low0, inv0, low1, inv1)

    perm = []
    for h in range(groups):
        for u in range(col_count):
            for v in range(col_count):
                source = (h * col_count + u) * col_count + v
                perm.append((source, (h * col_count + v) * col_count + u))
    swapped = lax.ppermute(payload, ("row", "col"), perm)
    pieces = [payload]
    for shift in range(1, col_count):
        ring = [(q, (q + shift) % col_count) for q in range(col_count)]
        pieces.append(lax.ppermute(payload, "col", ring))
    own = jnp.stack(pieces)
    across = lax.all_gather(swapped, "row")

    columns = jnp.arange(count, dtype=jnp.int32)
    turned = (col_index - columns + count * col_count) % col_count
    left = solve_panels(row_ids[:1], turned, own, factors, 1)
    right = solve_panels(col_ids[:groups], columns % col_count, across, factors, groups)
    out = update_tiles(row_ids, col_ids, marks, tiles, left, right)
    return out.reshape(matrix.shape)


def solution(mesh):
    return jax.shard_map(
        on_device,
        mesh=mesh,
        in_specs=(P(None, "row", None, "col", None, None), P(None, "row", None, "col")),
        out_specs=P(None, "row", None, "col", None, None),
        check_vma=False,
    )
```

profile of v0, /device:TPU:0, one launch (start us, length us, event | category | flops | bytes accessed | tf_op | source)
XLA Modules:
  0.0 215.3 jit_solution(4545458247570303971)
XLA Ops:
  6.5 0.0 copy-start.1
  6.5 0.0 all-gather.4.cloned.1.call-start
  6.5 0.8 copy.7
  7.3 1.2 reduce-precision_select_fusion
  8.5 0.1 broadcast_in_dim.15
  8.6 0.7 fusion
  9.3 0.0 all-gather.4.cloned.1.call-update
  9.3 0.0 all-gather.6.cloned.1.call-start
  9.3 0.1 fusion.2
  9.4 0.7 collective-permute-start.3
  10.2 0.0 collective-permute-done.3
  10.2 0.0 copy-start
  10.2 0.9 copy-done
  11.0 0.0 all-gather.6.cloned.1.call-update
  11.1 19.9 %collective-permute-start = (f32[5,2,136,128]{3,2,1,0:T(8,128)S(1)}, f32[5,2,136,128]{3,2,1,0:T(8,128)S(1)}, u32[]{:S(2)}, u32[]{:S(2)}) collective-permute-start(f32[5,2,136,128]{3,2,1,0:T(8,128)S(1)} %get-tuple-element.24), channel_id=1, source_target_pairs={{0,1},{1,2},{2,3},{3,0},{4,5},{5,6},{6,7},{7,4},{8,9},{9,10},{10,1... | collective-permute-start | bytes 2088968 | tf_op jit(solution)/shard_map/ppermute | solution.py:343
  31.0 6.4 %collective-permute-start.1 = (f32[5,2,136,128]{3,2,1,0:T(8,128)S(1)}, f32[5,2,136,128]{3,2,1,0:T(8,128)S(1)}, u32[]{:S(2)}, u32[]{:S(2)}) collective-permute-start(f32[5,2,136,128]{3,2,1,0:T(8,128)S(1)} %get-tuple-element.24), channel_id=1, source_target_pairs={{0,2},{1,3},{2,0},{3,1},{4,6},{5,7},{6,4},{7,5},{8,10},{9,11},{10,... | collective-permute-start | bytes 2088968 | tf_op jit(solution)/shard_map/ppermute | solution.py:343
  37.3 1.4 collective-permute-start.2
  38.7 0.0 copy-done.1
  38.8 0.7 reshape_reshape.3.refs_2_
  39.4 0.6 and_select_fusion.refs_1_
  40.0 0.5 multiply_add_fusion.refs_1_
  40.5 0.6 and_select_fusion.1.refs_1_
  41.0 0.5 multiply_add_fusion.1.refs_0_
  41.6 12.7 %collective-permute-done = f32[5,2,136,128]{3,2,1,0:T(8,128)S(1)} collective-permute-done((f32[5,2,136,128]{3,2,1,0:T(8,128)S(1)}, f32[5,2,136,128]{3,2,1,0:T(8,128)S(1)}, u32[]{:S(2)}, u32[]{:S(2)}) %collective-permute-start) | collective-permute-done | bytes 696352 | tf_op jit(solution)/shard_map/ppermute | solution.py:343
  54.2 1.6 collective-permute-done.1
  55.8 21.7 %collective-permute-done.2 = f32[5,2,136,128]{3,2,1,0:T(8,128)} collective-permute-done((f32[5,2,136,128]{3,2,1,0:T(8,128)S(1)}, f32[5,2,136,128]{3,2,1,0:T(8,128)}, u32[]{:S(2)}, u32[]{:S(2)}) %collective-permute-start.2) | collective-permute-done | bytes 696352 | tf_op jit(solution)/shard_map/ppermute | solution.py:343
  77.5 2.9 %pad_maximum_fusion.refs_2_ = f32[4,5,2,136,128]{4,3,2,1,0:T(8,128)} fusion(f32[1,5,2,136,128]{4,3,2,1,0:T(8,128)} %bitcast.4, f32[1,5,2,136,128]{4,3,2,1,0:T(8,128)S(1)} %bitcast.19, f32[1,5,2,136,128]{4,3,2,1,0:T(8,128)S(1)} %bitcast.18, f32[1,5,2,136,128]{4,3,2,1,0:T(8,128)S(1)} %get-tuple-element.23), kind=kLoop, calls=%fused_computation | loop fusion | flops 2088960 | bytes 5570560 | tf_op jit(solution)/shard_map/stack | solution.py:344
  80.4 4.7 %all-gather.4.cloned.1.call-done = f32[32,2,136,128]{3,2,1,0:T(8,128)} async-done(((f32[1,2,136,128]{3,2,1,0:T(8,128)}), f32[32,2,136,128]{3,2,1,0:T(8,128)}) %all-gather.4.cloned.1.call-update) | async-done | bytes 4456464 | tf_op jit(solution)/shard_map/all_gather | solution.py:327
  85.1 36.3 %factor_blocks.2 = (f32[1024,512]{1,0:T(8,128)}, f32[4,128,128]{2,1,0:T(8,128)}) custom-call(f32[8,4,2,136,128]{4,3,2,1,0:T(8,128)} %bitcast.24), custom_call_target="tpu_custom_call" | custom-call | flops 20000000000 | bytes 9000000 | tf_op jit(solution)/shard_map/factor_blocks/pallas_call | solution.py:135
  121.4 36.6 %factor_blocks.3 = (f32[512,512]{1,0:T(8,128)}, f32[4,128,128]{2,1,0:T(8,128)}) custom-call(f32[8,4,2,136,128]{4,3,2,1,0:T(8,128)} %bitcast.25, f32[1024,512]{1,0:T(8,128)} %get-tuple-element.13.refs_1_.refs_3_), custom_call_target="tpu_custom_call" | custom-call | flops 20000000000 | bytes 9000000 | tf_op jit(solution)/shard_map/factor_blocks/pallas_call | solution.py:135
  158.0 12.6 %solve_panels.2 = (bf16[1,640,1024]{2,1,0:T(8,128)(2,1)}, bf16[1,640,1024]{2,1,0:T(8,128)(2,1)}) custom-call(s32[1]{0:T(128)} %bitcast.22, s32[8]{0:T(128)} %and_select_fusion.1.refs_1_, f32[4,5,2,136,128]{4,3,2,1,0:T(8,128)} %pad_maximum_fusion.refs_2_, f32[1024,512]{1,0:T(8,128)} %get-tuple-element.13.refs_1_.refs_3_, ...), custom_call_target="tpu_custom_call" | custom-call | flops 4000000000 | bytes 6000000 | tf_op jit(solution)/shard_map/solve_panels/pallas_call | solution.py:217
  170.6 5.5 %all-gather.6.cloned.1.call-done = f32[40,2,136,128]{3,2,1,0:T(8,128)} async-done(((f32[5,2,136,128]{3,2,1,0:T(8,128)}), f32[40,2,136,128]{3,2,1,0:T(8,128)}) %all-gather.6.cloned.1.call-update) | async-done | bytes 5570576 | tf_op jit(solution)/shard_map/all_gather | solution.py:345
  176.1 19.1 %solve_panels.3 = (bf16[2,640,1024]{2,1,0:T(8,128)(2,1)}, bf16[2,640,1024]{2,1,0:T(8,128)(2,1)}) custom-call(s32[2]{0:T(128)} %bitcast.21, s32[8]{0:T(128)} %and_select_fusion.refs_1_, f32[8,5,2,136,128]{4,3,2,1,0:T(8,128)} %bitcast.23, f32[1024,512]{1,0:T(8,128)} %get-tuple-element.13.refs_1_.refs_3_, f32[4,128,128]{2,1,0:T(8,128)} %get-tuple-element.14.refs_4_, ...), custom_call_target="tpu_custom_call" | custom-call | flops 8000000000 | bytes 12000000 | tf_op jit(solution)/shard_map/solve_panels/pallas_call | solution.py:217
  195.2 13.2 %update_tiles.1 = f32[5,10,128,128]{3,2,1,0:T(8,128)} custom-call(s32[5]{0:T(128)} %multiply_add_fusion.1.refs_0_, s32[10]{0:T(128)} %multiply_add_fusion.refs_1_, s32[50]{0:T(128)} %reshape_reshape.3.refs_2_, f32[5,10,128,128]{3,2,1,0:T(8,128)} %bitcast.17, bf16[1,640,1024]{2,1,0:T(8,128)(2,1)} %get-tuple-element.17.refs_4_, ...), custom_call_target="tpu_custom_call" | custom-call | tf_op jit(solution)/shard_map/update_tiles/pallas_call | solution.py:291
  (2 shorter events, 0.0 us)
Async XLA Ops:
  6.5 32.2 %copy-start.1 = (s32[5,1,10,1]{2,3,1,0:T(1,128)S(1)}, s32[5,1,10,1]{2,3,1,0:T(1,128)}, u32[]{:S(2)}) copy-start(s32[5,1,10,1]{2,3,1,0:T(1,128)} %param.3) | copy-start | bytes 604
  6.5 78.6 %all-gather.4.cloned.1.call-start = ((), (), s32[]{:S(2)}) async-start(), calls=%async_computation | async-start | bytes 4595712 | tf_op jit(solution)/shard_map/all_gather | solution.py:327
  9.3 166.8 %all-gather.6.cloned.1.call-start = ((), (), s32[]{:S(2)}) async-start(), calls=%async_computation.1 | async-start | bytes 6266880 | tf_op jit(solution)/shard_map/all_gather | solution.py:345
  9.4 0.7 collective-permute-start.3
  10.2 0.9 copy-start
  11.1 43.2 %collective-permute-start = (f32[5,2,136,128]{3,2,1,0:T(8,128)S(1)}, f32[5,2,136,128]{3,2,1,0:T(8,128)S(1)}, u32[]{:S(2)}, u32[]{:S(2)}) collective-permute-start(f32[5,2,136,128]{3,2,1,0:T(8,128)S(1)} %get-tuple-element.24), channel_id=1, source_target_pairs={{0,1},{1,2},{2,3},{3,0},{4,5},{5,6},{6,7},{7,4},{8,9},{9,10},{10,1... | collective-permute-start | bytes 2088968 | tf_op jit(solution)/shard_map/ppermute | solution.py:343
  31.0 24.9 %collective-permute-start.1 = (f32[5,2,136,128]{3,2,1,0:T(8,128)S(1)}, f32[5,2,136,128]{3,2,1,0:T(8,128)S(1)}, u32[]{:S(2)}, u32[]{:S(2)}) collective-permute-start(f32[5,2,136,128]{3,2,1,0:T(8,128)S(1)} %get-tuple-element.24), channel_id=1, source_target_pairs={{0,2},{1,3},{2,0},{3,1},{4,6},{5,7},{6,4},{7,5},{8,10},{9,11},{10,... | collective-permute-start | bytes 2088968 | tf_op jit(solution)/shard_map/ppermute | solution.py:343
  37.3 40.2 %collective-permute-start.2 = (f32[5,2,136,128]{3,2,1,0:T(8,128)S(1)}, f32[5,2,136,128]{3,2,1,0:T(8,128)}, u32[]{:S(2)}, u32[]{:S(2)}) collective-permute-start(f32[5,2,136,128]{3,2,1,0:T(8,128)S(1)} %get-tuple-element.24), channel_id=1, source_target_pairs={{0,3},{1,0},{2,1},{3,2},{4,7},{5,4},{6,5},{7,6},{8,11},{9,8},{10,9... | collective-permute-start | bytes 2088968 | tf_op jit(solution)/shard_map/ppermute | solution.py:343
Sparse Core Ops, SparseCore 0:
  10.2 74.9 all-gather.3
  87.3 88.7 all-gather.5
where the time goes:
time: 216 us; the launch traced here: 215 us
  Pallas kernels  118 us (55%)
  waiting for transfers between devices  46.2 us (21%)
  starting transfers between devices  28.4 us (13%)
  between operations  13.4 us (6%)
  other arithmetic  7.05 us (3%)
  local copies, waits for them, and re-layouts  2.36 us (1%)
    pallas_call x2, Pallas kernels, factor_blocks(): pl.pallas_call(lambda *refs: factor_kernel(step, col_count, tile, *refs),...  72.9 us
    ppermute x3, waiting for transfers between devices, on_device(): pieces.append(lax.ppermute(payload, 'col', ring))  36 us
    pallas_call x2, Pallas kernels, solve_panels(): pl.pallas_call(lambda *refs: solve_kernel(tile, groups, *refs), grid_spec...  31.7 us
    ppermute x3, starting transfers between devices, on_device(): pieces.append(lax.ppermute(payload, 'col', ring))  27.7 us
    pallas_call x1, Pallas kernels, update_tiles(): pl.pallas_call(lambda *refs: update_kernel(tile, groups, *refs), grid_spe...  13.2 us
    all_gather x1, waiting for transfers between devices, on_device(): across = lax.all_gather(swapped, 'row')  5.51 us
    all_gather x1, waiting for transfers between devices, on_device(): grid = lax.all_gather(payload[0], ('row', 'col'))  4.7 us
  transfers between devices with their start and end apart: 6, of which 5 were waited for; matrix products, arithmetic and copies ran while one was open for 3% of the time, Pallas kernels for 40%

commit v1 on v0

--- a/solution.py
+++ b/solution.py
@@ -86,70 +86,290 @@
     lax.fori_loop(0, tile // MICRO, micro, 0)
 
 
-def factor_kernel(step, col_count, tile, grid_ref, *refs):
-    if step:
-        before_ref, low_ref, inv_ref, work_ref, up_ref = refs
-    else:
-        low_ref, inv_ref, work_ref, up_ref = refs
-    first = step * PT
-    count = 2 * PT - first
+def exchange_kernel(dims, p_ref, own_ref, across_ref, low0_ref, inv0_ref, low1_ref, inv1_ref,
+                    grid_ref, relay_ref, work_ref, up_ref,
+                    line_send, line_recv, spread_send, grid_recv, own_send, own_recv,
+                    column_send, across_recv, cross_send, result_send, result_recv, local_sem):
+    rows, cols, slots, skip, tile = dims
+    count = 2 * PT
+    groups = rows // cols
+    lines = rows // 2
+    row = lax.axis_index("row")
+    col = lax.axis_index("col")
+    along, side = row // 2, row % 2
+    wide, core = col // 2, col % 2
+    relays = (row + col) % 2 == 0
+    works = (row + col) % 2 == 1
+    partner = wide * 2 + 1 - core
+    bulk = p_ref.at[skip:]
+
+    def copy(src, dst, send, recv, to_row, to_col):
+        return pltpu.make_async_remote_copy(
+            src_ref=src, dst_ref=dst, send_sem=send, recv_sem=recv,
+            device_id=(to_row, to_col), device_id_type=pl.DeviceIdType.MESH,
+        )
+
+    def line_copies(act):
+        for s in range(slots):
+            for k in range(lines):
+                here = (k == along) & (core == side)
+
+                @pl.when((s * cols + col <= row) & (row < count) & jnp.logical_not(here))
+                def _():
+                    act(copy(p_ref.at[0, s], relay_ref.at[along, core, s], line_send.at[s, k],
+                             line_recv.at[along, core, s], 2 * k + side, wide * 2 + side))
+
+    def spread_copies(first, last, act, wait):
+        for k in range(first // 2, last // 2):
+            for c in range(2):
+                for s in range(slots):
+                    mine = (k == along) & (core == c)
+                    from_col = wide * 2 + c
+                    from_row = 2 * k + side
+                    need = s * cols + from_col <= from_row
+
+                    def targets(src):
+                        for n in range(2):
+                            for w in range(cols // 2):
+                                act(copy(src, grid_ref.at[from_row, from_col, s],
+                                         spread_send.at[k, c, s, n, w],
+                                         grid_recv.at[from_row, from_col, s],
+                                         2 * along + n, 2 * w + 1 - n))
+
+                    @pl.when(need & mine)
+                    def _():
+                        targets(p_ref.at[0, s])
+
+                    @pl.when(need & jnp.logical_not(mine))
+                    def _():
+                        if wait:
+                            copy(p_ref.at[0, s], relay_ref.at[k, c, s], line_send.at[s, 0],
+                                 line_recv.at[k, c, s], row, partner).wait_recv()
+                        targets(relay_ref.at[k, c, s])
+
+    def own_copies(act):
+        for k in range(1, cols):
+            act(copy(bulk, own_ref.at[col], own_send.at[k], own_recv.at[col], row, (col + k) % cols))
+
+    def column_copies(act):
+        for k in range(lines):
+            @pl.when(jnp.logical_not((k == along) & (col == row % cols)))
+            def _():
+                act(copy(bulk, across_ref.at[row // cols, col], column_send.at[k],
+                         across_recv.at[row // cols, col], 2 * k + side, row % cols))
+
+    def cross(act, wait):
+        near = jnp.clip((along - wide + cols // 4) // (cols // 2), 0, groups - 1)
+        for k in range(cols):
+            from_col = (wide + k // 2) % (cols // 2) * 2 + (core + k) % 2
+            for h in range(groups):
+                g = (near + h) % groups
+                mine = (g * cols + col == row) & (from_col == col)
+
+                def forward(src):
+                    return copy(src, across_ref.at[g, from_col], cross_send.at[g, from_col],
+                                across_recv.at[g, from_col], 2 * along + 1 - side, col)
+
+                @pl.when(mine)
+                def _():
+                    act(forward(bulk))
+
+                @pl.when(jnp.logical_not(mine))
+                def _():
+                    move = forward(across_ref.at[g, from_col])
+                    if wait:
+                        move.wait_recv()
+                    act(move)
+
+    def wait_grid(first, last):
+        for i in range(first, last):
+            for j in range(i + 1):
+                at = (i, j % cols, j // cols)
+                copy(p_ref.at[0, 0], grid_ref.at[at], line_send.at[0, 0], grid_recv.at[at], row, partner).wait_recv()
+
+    def wait_own():
+        for k in range(1, cols):
+            c = (col + k) % cols
+            copy(bulk, own_ref.at[c], own_send.at[k], own_recv.at[c], row, partner).wait_recv()
+
+    results = (low0_ref, inv0_ref, low1_ref, inv1_ref)
+
+    def result_copy(k):
+        return copy(results[k], results[k], result_send.at[k], result_recv.at[k], row, partner)
+
+    start = lambda move: move.start()
+    done = lambda move: move.wait_send()
+    keep = pltpu.make_async_copy(bulk, own_ref.at[col], local_sem.at[0])
+    keep_across = pltpu.make_async_copy(bulk, across_ref.at[row // cols, col], local_sem.at[1])
+    source = col == row % cols
+
+    line_copies(start)
+    keep.start()
+
+    @pl.when(source)
+    def _():
+        keep_across.start()
+
+    @pl.when(relays)
+    def _():
+        spread_copies(0, PT, start, True)
+        spread_copies(PT, count, start, True)
+        column_copies(start)
+        own_copies(start)
+        cross(start, True)
+
+    @pl.when(works)
+    def _():
+        wait_grid(0, PT)
+        column_copies(start)
+        own_copies(start)
+        factor_first(cols, tile, grid_ref, low0_ref, inv0_ref, work_ref, up_ref)
+        wait_grid(PT, count)
+        factor_rest(cols, tile, grid_ref, low0_ref, inv0_ref)
+        factor_second(cols, tile, grid_ref, low0_ref, low1_ref, inv1_ref, work_ref, up_ref)
+        for k in range(4):
+            result_copy(k).start()
+        for k in range(4):
+            result_copy(k).wait_send()
+        for g in range(groups):
+            for c in range(cols):
+                copy(bulk, across_ref.at[g, c], own_send.at[0], across_recv.at[g, c], row, partner).wait_recv()
+
+    line_copies(done)
+
+    @pl.when(relays)
+    def _():
+        spread_copies(0, count, done, False)
+        cross(done, False)
+        for k in range(4):
+            result_copy(k).wait_recv()
+
+    column_copies(done)
+    own_copies(done)
+    wait_own()
+    keep.wait()
+
+    @pl.when(source)
+    def _():
+        keep_across.wait()
+
+
+def span_of(tile):
+    return lambda i, j=None: slice(i * tile, (i + 1 if j is None else j) * tile)
+
+
+def load_piece(cols, tile, grid_ref, i, j):
     lane = lax.broadcasted_iota(jnp.int32, (tile, tile), 1)
     sub = lax.broadcasted_iota(jnp.int32, (tile, tile), 0)
-
-    def span(i, j=None):
-        return slice(i * tile, (i + 1 if j is None else j) * tile)
-
-    for i in range(count):
+    piece = grid_ref[i, j % cols, j // cols, 0:tile]
+    if i == j:
+        kept = jnp.where(lane <= sub, piece, 0.0)
+        piece = kept + jnp.where(lane < sub, piece, 0.0).T
+    return piece
+
+
+def factor_chain(tile, low_ref, inv_ref, work_ref, up_ref):
+    span = span_of(tile)
+    for t in range(PT):
+        factor_tile(low_ref[span(t), span(t)], work_ref, up_ref, inv_ref.at[t])
+        low_ref[span(t), span(t)] = up_ref[...].T
+        if t + 1 < PT:
+            solved = dot_nt(low_ref[span(t + 1, PT), span(t)], inv_ref[t])
+            low_ref[span(t + 1, PT), span(t)] = solved
+            for u in range(t + 1, PT):
+                low_ref[span(u, PT), span(u)] -= dot_nt(
+                    low_ref[span(u, PT), span(t)], low_ref[span(u), span(t)]
+                )
+
+
+def factor_first(cols, tile, grid_ref, low_ref, inv_ref, work_ref, up_ref):
+    span = span_of(tile)
+    for i in range(PT):
+        for j in range(PT):
+            if j > i:
+                low_ref[span(i), span(j)] = jnp.zeros((tile, tile), jnp.float32)
+            else:
+                low_ref[span(i), span(j)] = load_piece(cols, tile, grid_ref, i, j)
+    factor_chain(tile, low_ref, inv_ref, work_ref, up_ref)
+
+
+def factor_rest(cols, tile, grid_ref, low_ref, inv_ref):
+    span = span_of(tile)
+    rest = slice(PT * tile, 2 * PT * tile)
+    for i in range(PT, 2 * PT):
+        for j in range(PT):
+            low_ref[span(i), span(j)] = load_piece(cols, tile, grid_ref, i, j)
+    for t in range(PT):
+        value = low_ref[rest, span(t)]
+        if t:
+            value = value - dot_nt(low_ref[rest, span(0, t)], low_ref[span(t), span(0, t)])
+        low_ref[rest, span(t)] = dot_nt(value, inv_ref[t])
+
+
+def factor_second(cols, tile, grid_ref, before_ref, low_ref, inv_ref, work_ref, up_ref):
+    span = span_of(tile)
+    for i in range(PT):
         for j in range(PT):
             if j > i:
                 low_ref[span(i), span(j)] = jnp.zeros((tile, tile), jnp.float32)
                 continue
-            where = (first + i, (first + j) % col_count, (first + j) // col_count)
-            piece = grid_ref[(*where, slice(0, tile))]
-            if i == j:
-                kept = jnp.where(lane <= sub, piece, 0.0)
-                piece = kept + jnp.where(lane < sub, piece, 0.0).T
-            if step:
-                left = before_ref[span(PT + i), :]
-                right = before_ref[span(PT + j), :]
-                mark = grid_ref[(*where, slice(tile, tile + 1))]
-                piece = piece - jnp.where(mark > 0.5, dot_nt_coarse(left, right), dot_nt(left, right))
+            piece = load_piece(cols, tile, grid_ref, PT + i, PT + j)
+            left = before_ref[span(PT + i), :]
+            right = before_ref[span(PT + j), :]
+            at = PT + j
+            mark = grid_ref[PT + i, at % cols, at // cols, tile : tile + 1]
+            piece = piece - jnp.where(mark > 0.5, dot_nt_coarse(left, right), dot_nt(left, right))
             low_ref[span(i), span(j)] = piece
-    for t in range(PT):
-        factor_tile(low_ref[span(t), span(t)], work_ref, up_ref, inv_ref.at[t])
-        low_ref[span(t), span(t)] = up_ref[...].T
-        if t + 1 < count:
-            solved = dot_nt(low_ref[span(t + 1, count), span(t)], inv_ref[t])
-            low_ref[span(t + 1, count), span(t)] = solved
-            for u in range(t + 1, PT):
-                low_ref[span(u, count), span(u)] -= dot_nt(
-                    low_ref[span(u, count), span(t)], low_ref[span(u), span(t)]
-                )
-
-
-def factor_blocks(step, grid, *before):
-    col_count = grid.shape[1]
-    tile = grid.shape[4]
-    count = 2 * PT - step * PT
+    factor_chain(tile, low_ref, inv_ref, work_ref, up_ref)
+
+
+def exchange(payload, rows, cols):
+    tile_rows, slots, height, tile = payload.shape
+    count = 2 * PT
+    groups = rows // cols
+    skip = count // rows
+    dims = (rows, cols, slots, skip, tile)
+    part = (tile_rows - skip, slots, height, tile)
     vmem = pl.BlockSpec(memory_space=pltpu.VMEM)
+    hbm = pl.BlockSpec(memory_space=pltpu.HBM)
+    f32 = lambda *shape: jax.ShapeDtypeStruct(shape, jnp.float32)
+    dma = pltpu.SemaphoreType.DMA
     return pl.pallas_call(
-        lambda *refs: factor_kernel(step, col_count, tile, *refs),
+        lambda *refs: exchange_kernel(dims, *refs),
         out_shape=(
-            jax.ShapeDtypeStruct((count * tile, PT * tile), jnp.float32),
-            jax.ShapeDtypeStruct((PT, tile, tile), jnp.float32),
+            f32(cols, *part),
+            f32(groups, cols, *part),
+            f32(count * tile, PT * tile),
+            f32(PT, tile, tile),
+            f32(PT * tile, PT * tile),
+            f32(PT, tile, tile),
         ),
-        in_specs=[vmem] * (1 + len(before)),
-        out_specs=(vmem, vmem),
+        in_specs=[vmem],
+        out_specs=(hbm, hbm, vmem, vmem, vmem, vmem),
         scratch_shapes=[
+            pltpu.VMEM((count, cols, slots, height, tile), jnp.float32),
+            pltpu.VMEM((count // 2, 2, slots, height, tile), jnp.float32),
             pltpu.VMEM((tile, 2 * tile), jnp.float32),
             pltpu.VMEM((tile, tile), jnp.float32),
+            dma((slots, rows // 2)),
+            dma((count // 2, 2, slots)),
+            dma((count // 2, 2, slots, 2, cols // 2)),
+            dma((count, cols, slots)),
+            dma((cols,)),
+            dma((cols,)),
+            dma((rows // 2,)),
+            dma((groups, cols)),
+            dma((groups, cols)),
+            dma((4,)),
+            dma((4,)),
+            dma((2,)),
         ],
-        cost_estimate=pl.CostEstimate(flops=20_000_000_000, bytes_accessed=9_000_000, transcendentals=0),
-        name="factor_blocks",
-    )(grid, *before)
-
-
-def solve_kernel(tile, groups, ids_ref, order_ref, panel_ref, low0_ref, inv0_ref, low1_ref, inv1_ref,
+        compiler_params=pltpu.CompilerParams(has_side_effects=True, vmem_limit_bytes=32 * 1024 * 1024),
+        name="exchange",
+    )(payload)
+
+
+def solve_kernel(tile, skip, ids_ref, order_ref, panel_ref, low0_ref, inv0_ref, low1_ref, inv1_ref,
                  high_ref, rest_ref, low_h, low_l, inv_h, inv_l):
     count = 2 * PT
     width = PT * tile
@@ -175,13 +395,15 @@
     def flat(value):
         return value.reshape(rows * tile, tile)
 
+    mine = slice(skip * tile, (skip + rows) * tile)
+
     for t in range(count):
         first = t // PT * PT
         slot = t // col_count
         owner = order_ref[t]
         value = flat(panel_ref[owner, :, slot, :tile, :])
         if first:
-            left = (high_ref[0, :, :width], rest_ref[0, :, :width])
+            left = (high_ref[0, mine, :width], rest_ref[0, mine, :width])
             right = (low_h[span(t), :width], low_l[span(t), :width])
             coarse = dot_bf16(left[0], right[0])
             exact = coarse + (dot_bf16(left[0], right[1]) + dot_bf16(left[1], right[0]))
@@ -190,10 +412,10 @@
             value = value - jnp.where(mark > 0.5, coarse, exact)
         if t > first:
             value = value - dot_pairs(
-                (high_ref[0, :, span(first, t)], rest_ref[0, :, span(first, t)]),
+                (high_ref[0, mine, span(first, t)], rest_ref[0, mine, span(first, t)]),
                 (low_h[span(t), span(first, t)], low_l[span(t), span(first, t)]),
             )
-        high_ref[0, :, span(t)], rest_ref[0, :, span(t)] = split(
+        high_ref[0, mine, span(t)], rest_ref[0, mine, span(t)] = split(
             dot_pairs(split(value), (inv_h[t], inv_l[t]))
         )
 
@@ -206,16 +428,16 @@
         rest_ref[0, :tile, :] = low_l[pl.ds(base, tile), :]
 
 
-def solve_panels(ids, order, panels, factors, groups):
+def solve_panels(ids, order, panels, factors, groups, skip):
     col_count = panels.shape[0] // groups
     _, rows, slots, height, tile = panels.shape
     count = 2 * PT
     full = count * tile
     keep = lambda n: (lambda g, *refs: (0,) * n)
-    out_spec = pl.BlockSpec((1, rows * tile, full), lambda g, *refs: (g, 0, 0))
-    out_shape = jax.ShapeDtypeStruct((groups, rows * tile, full), jnp.bfloat16)
+    out_spec = pl.BlockSpec((1, (skip + rows) * tile, full), lambda g, *refs: (g, 0, 0))
+    out_shape = jax.ShapeDtypeStruct((groups, (skip + rows) * tile, full), jnp.bfloat16)
     return pl.pallas_call(
-        lambda *refs: solve_kernel(tile, groups, *refs),
+        lambda *refs: solve_kernel(tile, skip, *refs),
         grid_spec=pltpu.PrefetchScalarGridSpec(
             num_scalar_prefetch=2,
             grid=(groups,),
@@ -324,30 +546,12 @@
     tags = jnp.broadcast_to(head_marks.astype(jnp.float32), (tile_rows, slots, 8, tile))
     payload = jnp.concatenate([stored, tags], axis=2)
 
-    grid = lax.all_gather(payload[0], ("row", "col"))
-    grid = grid.reshape(row_count, col_count, slots, tile + 8, tile)[:count]
-    low0, inv0 = factor_blocks(0, grid)
-    low1, inv1 = factor_blocks(1, grid, low0)
-    factors = (low0, inv0, low1, inv1)
-
-    perm = []
-    for h in range(groups):
-        for u in range(col_count):
-            for v in range(col_count):
-                source = (h * col_count + u) * col_count + v
-                perm.append((source, (h * col_count + v) * col_count + u))
-    swapped = lax.ppermute(payload, ("row", "col"), perm)
-    pieces = [payload]
-    for shift in range(1, col_count):
-        ring = [(q, (q + shift) % col_count) for q in range(col_count)]
-        pieces.append(lax.ppermute(payload, "col", ring))
-    own = jnp.stack(pieces)
-    across = lax.all_gather(swapped, "row")
-
+    own, across, *factors = exchange(payload, row_count, col_count)
+    skip = count // row_count
     columns = jnp.arange(count, dtype=jnp.int32)
-    turned = (col_index - columns + count * col_count) % col_count
-    left = solve_panels(row_ids[:1], turned, own, factors, 1)
-    right = solve_panels(col_ids[:groups], columns % col_count, across, factors, groups)
+    across = across.reshape(groups * col_count, *across.shape[2:])
+    left = solve_panels(row_ids[:1], columns % col_count, own, factors, 1, skip)
+    right = solve_panels(col_ids[:groups], columns % col_count, across, factors, groups, skip)
     out = update_tiles(row_ids, col_ids, marks, tiles, left, right)
     return out.reshape(matrix.shape)
 

time: 216 us -> 176 us (0.81)
  the two profiles are of different devices: /device:TPU:0 before, /device:TPU:9 now
where the time goes in v1:
time: 176 us
  Pallas kernels  164 us (93%)
  local copies, waits for them, and re-layouts  8.55 us (5%)
  other arithmetic  2.85 us (2%)
    pallas_call x1, Pallas kernels, exchange(): pl.pallas_call(lambda *refs: exchange_kernel(dims, *refs), out_shape=(f32...  123 us
    pallas_call x2, Pallas kernels, solve_panels(): pl.pallas_call(lambda *refs: solve_kernel(tile, skip, *refs), grid_spec=p...  27.9 us
    pallas_call x1, Pallas kernels, update_tiles(): pl.pallas_call(lambda *refs: update_kernel(tile, groups, *refs), grid_spe...  13.2 us
    unnamed x15, local copies, waits for them, and re-layouts  7.8 us

profile of v1, /device:TPU:9, one launch (start us, length us, event | category | flops | bytes accessed | tf_op | source)
XLA Modules:
  0.0 175.8 jit_solution(15452902449689267153)
XLA Ops:
  0.0 0.7 copy.6
  0.7 1.2 reduce-precision_select_fusion
  1.9 0.1 broadcast_in_dim.15
  2.0 0.1 pad_maximum_fusion.refs_0_
  2.0 123.3 %exchange.1 = (f32[4,4,2,136,128]{4,3,2,1,0:T(8,128)S(1)}, f32[2,4,4,2,136,128]{5,4,3,2,1,0:T(8,128)S(1)}, f32[1024,512]{1,0:T(8,128)S(1)}, f32[4,128,128]{2,1,0...) custom-call(f32[5,2,136,128]{3,2,1,0:T(8,128)S(1)} %pad_maximum_fusion.refs_0_), custom_call_target="tpu_custom_call" | custom-call | tf_op jit(solution)/shard_map/exchange/pallas_call | solution.py:337
  125.3 0.0 copy-start
  125.3 2.0 %copy-done = f32[2,4,4,2,136,128]{5,4,3,2,1,0:T(8,128)} copy-done((f32[2,4,4,2,136,128]{5,4,3,2,1,0:T(8,128)}, f32[2,4,4,2,136,128]{5,4,3,2,1,0:T(8,128)S(1)}, u32[]{:S(2)}) %copy-start) | copy-done | bytes 4456472
  127.3 0.0 copy-start.1
  127.3 1.4 copy-done.1
  128.7 0.0 copy-start.2
  128.7 1.3 copy-done.2
  130.0 0.0 copy-start.3
  130.0 1.0 copy-done.3
  131.0 0.0 copy-start.4
  131.0 0.7 copy-done.4
  131.7 0.0 copy-start.5
  131.7 0.7 copy-done.5
  132.4 0.5 multiply_add_fusion.refs_1_
  133.0 0.5 and_select_fusion.refs_1_
  133.5 16.6 %solve_panels.3 = (bf16[2,640,1024]{2,1,0:T(8,128)(2,1)}, bf16[2,640,1024]{2,1,0:T(8,128)(2,1)}) custom-call(s32[2]{0:T(128)} %bitcast.14, s32[8]{0:T(128)} %and_select_fusion.refs_1_, f32[8,4,2,136,128]{4,3,2,1,0:T(8,128)} %bitcast.10, f32[1024,512]{1,0:T(8,128)} %copy-done.2, f32[4,128,128]{2,1,0:T(8,128)} %copy-done.4, f32[512,512]{1,0:T(8,128)} %copy-done.3, ...), custom_call_target="tpu_custom_call" | custom-call | flops 8000000000 | bytes 12000000 | tf_op jit(solution)/shard_map/solve_panels/pallas_call | solution.py:439
  150.1 0.5 multiply_add_fusion.1.refs_0_
  150.6 0.0 copy-start.6
  150.6 11.4 %solve_panels.2 = (bf16[1,640,1024]{2,1,0:T(8,128)(2,1)}, bf16[1,640,1024]{2,1,0:T(8,128)(2,1)}) custom-call(s32[1]{0:T(128)} %bitcast.15, s32[8]{0:T(128)} %and_select_fusion.refs_1_, f32[4,4,2,136,128]{4,3,2,1,0:T(8,128)} %copy-done.1, f32[1024,512]{1,0:T(8,128)} %copy-done.2, f32[4,128,128]{2,1,0:T(8,128)} %copy-done.4, f32[512,512]{1,0:T(8,128)} %copy-done.3, ...), custom_call_target="tpu_custom_call" | custom-call | flops 4000000000 | bytes 6000000 | tf_op jit(solution)/shard_map/solve_panels/pallas_call | solution.py:439
  162.0 0.0 copy-done.6
  162.0 0.7 reshape_reshape.3.refs_2_
  162.6 13.2 %update_tiles.1 = f32[5,10,128,128]{3,2,1,0:T(8,128)} custom-call(s32[5]{0:T(128)} %multiply_add_fusion.1.refs_0_, s32[10]{0:T(128)} %multiply_add_fusion.refs_1_, s32[50]{0:T(128)} %reshape_reshape.3.refs_2_, f32[5,10,128,128]{3,2,1,0:T(8,128)} %bitcast.12, bf16[1,640,1024]{2,1,0:T(8,128)(2,1)} %get-tuple-element.20.refs_4_, ...), custom_call_target="tpu_custom_call" | custom-call | tf_op jit(solution)/shard_map/update_tiles/pallas_call | solution.py:513
  (2 shorter events, 0.0 us)
Async XLA Ops:
  125.3 2.0 %copy-start = (f32[2,4,4,2,136,128]{5,4,3,2,1,0:T(8,128)}, f32[2,4,4,2,136,128]{5,4,3,2,1,0:T(8,128)S(1)}, u32[]{:S(2)}) copy-start(f32[2,4,4,2,136,128]{5,4,3,2,1,0:T(8,128)S(1)} %get-tuple-element.22) | copy-start | bytes 13369348
  127.3 1.4 copy-start.1
  128.7 1.3 copy-start.2
  130.0 1.0 copy-start.3
  131.0 0.7 copy-start.4
  131.7 0.7 copy-start.5
  150.6 11.4 %copy-start.6 = (s32[5,1,10,1]{2,3,1,0:T(1,128)S(1)}, s32[5,1,10,1]{2,3,1,0:T(1,128)}, u32[]{:S(2)}) copy-start(s32[5,1,10,1]{2,3,1,0:T(1,128)} %param.3) | copy-start | bytes 604

commit v2 on v1

v2 whole, which is shorter than its diff:
```python
import jax
import jax.numpy as jnp
from jax import lax
from jax.experimental import pallas as pl
from jax.experimental.pallas import tpu as pltpu
from jax.sharding import PartitionSpec as P

PT = 4
MICRO = 32
NT_DIMS = (((1,), (1,)), ((), ()))
TN_DIMS = (((0,), (0,)), ((), ()))


def dot_nt_coarse(a, b):
    return lax.dot_general(
        a.astype(jnp.bfloat16),
        b.astype(jnp.bfloat16),
        NT_DIMS,
        preferred_element_type=jnp.float32,
    )


def split(value):
    high = value.astype(jnp.bfloat16)
    return high, (value - high.astype(jnp.float32)).astype(jnp.bfloat16)


def dot_bf16(a, b):
    return lax.dot_general(a, b, NT_DIMS, preferred_element_type=jnp.float32)


def split3(value):
    high = value.astype(jnp.bfloat16)
    rest = value - high.astype(jnp.float32)
    mid = rest.astype(jnp.bfloat16)
    return high, mid, (rest - mid.astype(jnp.float32)).astype(jnp.bfloat16)


def wide_nt(a, b):
    ah, am, al = split3(a)
    bh, bm, bl = split3(b)
    left = jnp.concatenate([ah, ah, am, am, ah, al], axis=1)
    right = jnp.concatenate([bh, bm, bh, bm, bl, bh], axis=1)
    return dot_bf16(left, right)


def factor_tile(work_ref, low_ref, upper_ref, inv_ref):
    tile = work_ref.shape[0]
    lanes = lax.broadcasted_iota(jnp.int32, (8, tile), 1)
    subs = lax.broadcasted_iota(jnp.int32, (8, tile), 0)
    parts = MICRO // 8

    def spread(value, k):
        return jnp.broadcast_to(value[k : k + 1, :], (8, tile))

    for base in range(0, tile, MICRO):
        raw = {g: work_ref[base + 8 * g : base + 8 * g + 8, :] for g in range(parts)}
        col, slab, diag = {}, {}, {}
        for g in range(parts):
            for q in range(8 * g + 8):
                col[q, g] = jnp.broadcast_to(raw[g][:, base + q : base + q + 1], (8, tile))
            inside = (lanes >= base) & (lanes < base + MICRO)
            one = (lanes == base + 8 * g + subs).astype(jnp.float32)
            slab[g] = jnp.where(inside, one, raw[g])
            diag[g] = jnp.zeros((8, tile), jnp.float32)
        for q in range(0, MICRO, 2):
            h, k = q // 8, q % 8
            d0 = spread(col[q, h], k)
            e = spread(col[q, h], k + 1)
            d1 = spread(col[q + 1, h], k + 1)
            r0 = lax.rsqrt(d0)
            r1 = lax.rsqrt(d0 * d1 - e * e) * (d0 * r0)
            l10 = e * r0
            l0, l1 = {}, {}
            for g in range(h, parts):
                l0[g] = col[q, g] * r0
                l1[g] = (col[q + 1, g] - l0[g] * l10) * r1
                diag[g] = jnp.where(lanes == base + q, l0[g], jnp.where(lanes == base + q + 1, l1[g], diag[g]))
            for m in range(q + 2, MICRO):
                a0 = spread(l0[m // 8], m % 8)
                a1 = spread(l1[m // 8], m % 8)
                for g in range(m // 8, parts):
                    col[m, g] = col[m, g] - (l0[g] * a0 + l1[g] * a1)
            u0 = spread(slab[h], k) * r0
            u1 = (spread(slab[h], k + 1) - u0 * l10) * r1
            for g in range(h, parts):
                new = slab[g] - (l0[g] * u0 + l1[g] * u1)
                if g == h:
                    old = jnp.where(subs == k, u0, slab[g])
                    new = jnp.where(subs > k + 1, new, jnp.where(subs == k + 1, u1, old))
                slab[g] = new
        for g in range(parts):
            at = slice(base + 8 * g, base + 8 * g + 8)
            under = lanes <= base + 8 * g + subs
            low_ref[at, :] = jnp.where(under, diag[g], 0.0)
            upper_ref[at, :] = jnp.where(lanes >= base + MICRO, slab[g], 0.0)
            inv_ref[at, :] = jnp.where(under, slab[g], 0.0)
        if base + MICRO < tile:
            high, mid, rest = split3(jnp.concatenate([slab[g] for g in range(parts)], axis=0))
            left = jnp.concatenate([high, high, mid, mid, high, rest], axis=0)
            right = jnp.concatenate([high, mid, high, mid, rest, high], axis=0)
            after = slice(base + MICRO, tile)
            outer = lax.dot_general(left, right, TN_DIMS, preferred_element_type=jnp.float32)[after]
            lane = lax.broadcasted_iota(jnp.int32, (tile - base - MICRO, tile), 1)
            inside = (lane >= base) & (lane < base + MICRO)
            work_ref[after, :] = jnp.where(inside, 0.0, work_ref[after, :]) - outer
    low_ref[...] += upper_ref[...].T


def exchange_kernel(dims, p_ref, own_ref, across_ref, low0_ref, inv0_ref, low1_ref, inv1_ref,
                    grid_ref, relay_ref, work_ref, up_ref,
                    line_send, line_recv, spread_send, grid_recv, own_send, own_recv,
                    column_send, across_recv, cross_send, result_send, result_recv, local_sem):
    rows, cols, slots, skip, tile = dims
    count = 2 * PT
    groups = rows // cols
    lines = rows // 2
    row = lax.axis_index("row")
    col = lax.axis_index("col")
    along, side = row // 2, row % 2
    wide, core = col // 2, col % 2
    relays = (row + col) % 2 == 0
    works = (row + col) % 2 == 1
    partner = wide * 2 + 1 - core
    bulk = p_ref.at[skip:]

    def copy(src, dst, send, recv, to_row, to_col):
        return pltpu.make_async_remote_copy(
            src_ref=src, dst_ref=dst, send_sem=send, recv_sem=recv,
            device_id=(to_row, to_col), device_id_type=pl.DeviceIdType.MESH,
        )

    def line_copies(act):
        for s in range(slots):
            for k in range(lines):
                here = (k == along) & (core == side)

                @pl.when((s * cols + col <= row) & (row < count) & jnp.logical_not(here))
                def _():
                    act(copy(p_ref.at[0, s], relay_ref.at[along, core, s], line_send.at[s, k],
                             line_recv.at[along, core, s], 2 * k + side, wide * 2 + side))

    def spread_copies(first, last, act, wait):
        for k in range(first // 2, last // 2):
            for c in range(2):
                for s in range(slots):
                    mine = (k == along) & (core == c)
                    from_col = wide * 2 + c
                    from_row = 2 * k + side
                    need = s * cols + from_col <= from_row

                    def targets(src):
                        for n in range(2):
                            for w in range(cols // 2):
                                act(copy(src, grid_ref.at[from_row, from_col, s],
                                         spread_send.at[k, c, s, n, w],
                                         grid_recv.at[from_row, from_col, s],
                                         2 * along + n, 2 * w + 1 - n))

                    @pl.when(need & mine)
                    def _():
                        targets(p_ref.at[0, s])

                    @pl.when(need & jnp.logical_not(mine))
                    def _():
                        if wait:
                            copy(p_ref.at[0, s], relay_ref.at[k, c, s], line_send.at[s, 0],
                                 line_recv.at[k, c, s], row, partner).wait_recv()
                        targets(relay_ref.at[k, c, s])

    def own_copies(act):
        for k in range(1, cols):
            act(copy(bulk, own_ref.at[col], own_send.at[k], own_recv.at[col], row, (col + k) % cols))

    def column_copies(act):
        for k in range(lines):
            @pl.when(jnp.logical_not((k == along) & (col == row % cols)))
            def _():
                act(copy(bulk, across_ref.at[row // cols, col], column_send.at[k],
                         across_recv.at[row // cols, col], 2 * k + side, row % cols))

    def cross(act, wait):
        near = jnp.clip((along - wide + cols // 4) // (cols // 2), 0, groups - 1)
        for k in range(cols):
            from_col = (wide + k // 2) % (cols // 2) * 2 + (core + k) % 2
            for h in range(groups):
                g = (near + h) % groups
                mine = (g * cols + col == row) & (from_col == col)

                def forward(src):
                    return copy(src, across_ref.at[g, from_col], cross_send.at[g, from_col],
                                across_recv.at[g, from_col], 2 * along + 1 - side, col)

                @pl.when(mine)
                def _():
                    act(forward(bulk))

                @pl.when(jnp.logical_not(mine))
                def _():
                    move = forward(across_ref.at[g, from_col])
                    if wait:
                        move.wait_recv()
                    act(move)

    def wait_grid(first, last):
        for i in range(first, last):
            for j in range(i + 1):
                at = (i, j % cols, j // cols)
                copy(p_ref.at[0, 0], grid_ref.at[at], line_send.at[0, 0], grid_recv.at[at], row, partner).wait_recv()

    def wait_own():
        for k in range(1, cols):
            c = (col + k) % cols
            copy(bulk, own_ref.at[c], own_send.at[k], own_recv.at[c], row, partner).wait_recv()

    results = (low0_ref, inv0_ref, low1_ref, inv1_ref)

    def result_copy(k):
        return copy(results[k], results[k], result_send.at[k], result_recv.at[k], row, partner)

    start = lambda move: move.start()
    done = lambda move: move.wait_send()
    keep = pltpu.make_async_copy(bulk, own_ref.at[col], local_sem.at[0])
    keep_across = pltpu.make_async_copy(bulk, across_ref.at[row // cols, col], local_sem.at[1])
    source = col == row % cols

    line_copies(start)
    keep.start()

    @pl.when(source)
    def _():
        keep_across.start()

    @pl.when(relays)
    def _():
        spread_copies(0, PT, start, True)
        spread_copies(PT, count, start, True)
        column_copies(start)
        own_copies(start)
        cross(start, True)

    @pl.when(works)
    def _():
        wait_grid(0, PT)
        column_copies(start)
        own_copies(start)
        factor_first(cols, tile, grid_ref, low0_ref, inv0_ref, work_ref, up_ref)
        wait_grid(PT, count)
        factor_rest(cols, tile, grid_ref, low0_ref, inv0_ref)
        factor_second(cols, tile, grid_ref, low0_ref, low1_ref, inv1_ref, work_ref, up_ref,
                      lambda: [result_copy(k).start() for k in range(2)])
        for k in range(2, 4):
            result_copy(k).start()
        for k in range(4):
            result_copy(k).wait_send()
        for g in range(groups):
            for c in range(cols):
                copy(bulk, across_ref.at[g, c], own_send.at[0], across_recv.at[g, c], row, partner).wait_recv()

    line_copies(done)

    @pl.when(relays)
    def _():
        spread_copies(0, count, done, False)
        cross(done, False)
        for k in range(4):
            result_copy(k).wait_recv()

    column_copies(done)
    own_copies(done)
    wait_own()
    keep.wait()

    @pl.when(source)
    def _():
        keep_across.wait()


def span_of(tile):
    return lambda i, j=None: slice(i * tile, (i + 1 if j is None else j) * tile)


def load_piece(cols, tile, grid_ref, i, j):
    lane = lax.broadcasted_iota(jnp.int32, (tile, tile), 1)
    sub = lax.broadcasted_iota(jnp.int32, (tile, tile), 0)
    piece = grid_ref[i, j % cols, j // cols, 0:tile]
    if i == j:
        kept = jnp.where(lane <= sub, piece, 0.0)
        piece = kept + jnp.where(lane < sub, piece, 0.0).T
    return piece


def factor_chain(tile, low_ref, inv_ref, work_ref, up_ref):
    span = span_of(tile)
    for t in range(PT):
        pair, half = t // 2, t % 2
        at = span(half)
        work_ref[...] = low_ref[span(t), span(t)]
        factor_tile(work_ref, low_ref.at[span(t), span(t)], up_ref, inv_ref.at[pair, at, at])
        if t + 1 < PT:
            solved = wide_nt(low_ref[span(t + 1, PT), span(t)], inv_ref[pair, at, at])
            low_ref[span(t + 1, PT), span(t)] = solved
            for u in range(t + 1, PT):
                low_ref[span(u, PT), span(u)] -= wide_nt(
                    low_ref[span(u, PT), span(t)], low_ref[span(u), span(t)]
                )
        if half:
            under = wide_nt(inv_ref[pair, at, at], low_ref[span(t), span(t - 1)].T)
            inv_ref[pair, at, span(0)] = -wide_nt(under, inv_ref[pair, span(0), span(0)].T)
            inv_ref[pair, span(0), at] = jnp.zeros((tile, tile), jnp.float32)


def factor_first(cols, tile, grid_ref, low_ref, inv_ref, work_ref, up_ref):
    span = span_of(tile)
    for i in range(PT):
        for j in range(PT):
            if j > i:
                low_ref[span(i), span(j)] = jnp.zeros((tile, tile), jnp.float32)
            else:
                low_ref[span(i), span(j)] = load_piece(cols, tile, grid_ref, i, j)
    factor_chain(tile, low_ref, inv_ref, work_ref, up_ref)


def factor_rest(cols, tile, grid_ref, low_ref, inv_ref):
    span = span_of(tile)
    rest = slice(PT * tile, 2 * PT * tile)
    for i in range(PT, 2 * PT):
        for j in range(PT):
            low_ref[span(i), span(j)] = load_piece(cols, tile, grid_ref, i, j)
    for t in range(PT):
        value = low_ref[rest, span(t)]
        if t:
            value = value - wide_nt(low_ref[rest, span(0, t)], low_ref[span(t), span(0, t)])
        at = span(t % 2)
        low_ref[rest, span(t)] = wide_nt(value, inv_ref[t // 2, at, at])


def factor_second(cols, tile, grid_ref, before_ref, low_ref, inv_ref, work_ref, up_ref, ready):
    span = span_of(tile)
    for i in range(PT):
        for j in range(PT):
            if j > i:
                low_ref[span(i), span(j)] = jnp.zeros((tile, tile), jnp.float32)
                continue
            piece = load_piece(cols, tile, grid_ref, PT + i, PT + j)
            left = before_ref[span(PT + i), :]
            right = before_ref[span(PT + j), :]
            at = PT + j
            mark = grid_ref[PT + i, at % cols, at // cols, tile : tile + 1]
            exact = wide_nt(left[:, : 2 * tile], right[:, : 2 * tile]) + wide_nt(left[:, 2 * tile :], right[:, 2 * tile :])
            piece = piece - jnp.where(mark > 0.5, dot_nt_coarse(left, right), exact)
            low_ref[span(i), span(j)] = piece
    ready()
    factor_chain(tile, low_ref, inv_ref, work_ref, up_ref)


def exchange(payload, rows, cols):
    tile_rows, slots, height, tile = payload.shape
    count = 2 * PT
    groups = rows // cols
    skip = count // rows
    dims = (rows, cols, slots, skip, tile)
    part = (tile_rows - skip, slots, height, tile)
    vmem = pl.BlockSpec(memory_space=pltpu.VMEM)
    hbm = pl.BlockSpec(memory_space=pltpu.HBM)
    f32 = lambda *shape: jax.ShapeDtypeStruct(shape, jnp.float32)
    dma = pltpu.SemaphoreType.DMA
    return pl.pallas_call(
        lambda *refs: exchange_kernel(dims, *refs),
        out_shape=(
            f32(cols, *part),
            f32(groups, cols, *part),
            f32(count * tile, PT * tile),
            f32(PT // 2, 2 * tile, 2 * tile),
            f32(PT * tile, PT * tile),
            f32(PT // 2, 2 * tile, 2 * tile),
        ),
        in_specs=[vmem],
        out_specs=(hbm, hbm, vmem, vmem, vmem, vmem),
        scratch_shapes=[
            pltpu.VMEM((count, cols, slots, height, tile), jnp.float32),
            pltpu.VMEM((count // 2, 2, slots, height, tile), jnp.float32),
            pltpu.VMEM((tile, tile), jnp.float32),
            pltpu.VMEM((tile, tile), jnp.float32),
            dma((slots, rows // 2)),
            dma((count // 2, 2, slots)),
            dma((count // 2, 2, slots, 2, cols // 2)),
            dma((count, cols, slots)),
            dma((cols,)),
            dma((cols,)),
            dma((rows // 2,)),
            dma((groups, cols)),
            dma((groups, cols)),
            dma((4,)),
            dma((4,)),
            dma((2,)),
        ],
        compiler_params=pltpu.CompilerParams(has_side_effects=True, vmem_limit_bytes=32 * 1024 * 1024),
        name="exchange",
    )(payload)


def finish_kernel(row_count, marks_ref, tiles_ref, own_ref, across_ref, low0_hbm, inv0_hbm, low1_hbm, inv1_hbm,
                  out_ref, panel_ref, low0_ref, inv0_ref, low1_ref, inv1_ref, inv_ref, under_ref, cross_h, cross_l,
                  high_ref, rest_ref, raw_ref, new_ref, factor_sem, panel_sem, raw_sem, new_sem):
    groups, col_count, rows, slots, height, tile = across_ref.shape
    tile_rows, tile_cols = tiles_ref.shape[:2]
    count = 2 * PT
    width = PT * tile
    size = rows * tile
    skip = tile_rows - rows
    first_col = count // col_count
    row = lax.axis_index("row")
    col = lax.axis_index("col")
    span = span_of(tile)

    factor_copies = [
        pltpu.make_async_copy(src, dst, factor_sem.at[k])
        for k, (src, dst) in enumerate(
            ((inv0_hbm, inv0_ref), (low0_hbm, low0_ref), (inv1_hbm, inv1_ref), (low1_hbm, low1_ref))
        )
    ]
    panel_copies = [pltpu.make_async_copy(own_ref, panel_ref.at[0], panel_sem.at[0])] + [
        pltpu.make_async_copy(across_ref.at[g], panel_ref.at[1 + g], panel_sem.at[1 + g]) for g in range(groups)
    ]
    raw_copy = pltpu.make_async_copy(tiles_ref, raw_ref, raw_sem)
    for move in (factor_copies[0], panel_copies[0], *factor_copies[1:], *panel_copies[1:], raw_copy):
        move.start()

    def stacked(value):
        high, rest = split(value)
        return jnp.concatenate([high, high, rest], axis=1)

    def dot_stacked(value, weights):
        high, rest = split(value)
        return dot_bf16(jnp.concatenate([high, rest, high], axis=1), weights)

    for move in factor_copies:
        move.wait()
    for k in range(PT // 2):
        inv_ref[k] = stacked(inv0_ref[k])
        inv_ref[PT // 2 + k] = stacked(inv1_ref[k])
    for k, ref in enumerate((low0_ref, low1_ref)):
        for n in range(1, PT // 2):
            under_ref[k, n - 1] = stacked(ref[span(2 * n, 2 * n + 2), span(0, 2)])
    cross_h[...], cross_l[...] = split(low0_ref[span(PT, count), :])

    def solve(group, carry):
        pltpu.make_async_copy(own_ref, panel_ref.at[group], panel_sem.at[group]).wait()

        def column(t):
            return panel_ref[group, t % col_count, :, t // col_count, :tile, :].reshape(size, tile)

        def mark(t):
            value = panel_ref[group, t % col_count, :, t // col_count, tile : tile + 1, :]
            return jnp.broadcast_to(value, (rows, tile, tile)).reshape(size, tile)

        def keep(at, value):
            high_ref[group, :, at], rest_ref[group, :, at] = split(value)

        for p in range(2):
            done = None
            for n in range(PT // 2):
                t = p * PT + 2 * n
                value = jnp.concatenate([column(t), column(t + 1)], axis=1)
                if p:
                    high, rest = high_ref[group, :, :width], rest_ref[group, :, :width]
                    at = span(2 * n, 2 * n + 2)
                    coarse = dot_bf16(high, cross_h[at, :])
                    more = dot_bf16(high, cross_l[at, :]) + dot_bf16(rest, cross_h[at, :])
                    marks = jnp.concatenate([mark(t), mark(t + 1)], axis=1)
                    value = value - (coarse + jnp.where(marks > 0.5, 0.0, more))
                if n:
                    value = value - dot_stacked(done, under_ref[p, n - 1])
                done = dot_stacked(value, inv_ref[p * (PT // 2) + n])
                keep(span(t, t + 2), done)
        return carry

    lax.fori_loop(0, 1 + groups, solve, 0)

    def rounded(value):
        return value.astype(jnp.bfloat16).astype(jnp.float32)

    def write(a, c):
        return pltpu.make_async_copy(new_ref.at[a, c], out_ref.at[a, c], new_sem.at[a, c])

    def panel_tile(a, c):
        base = pl.multiple_of((c * col_count + col) * tile, tile)
        is_bf16 = marks_ref[a, c] == 1
        if a >= skip:
            at = slice((a - skip) * tile, (a - skip + 1) * tile)
            rest = rest_ref[0, at, pl.ds(base, tile)].astype(jnp.float32)
            new_ref[a, c] = high_ref[0, at, pl.ds(base, tile)].astype(jnp.float32) + jnp.where(is_bf16, 0.0, rest)
        if a * row_count < count:
            @pl.when(row < count)
            def _():
                place = pl.multiple_of(jnp.minimum(row, count - 1) * tile, tile)
                inner = c * col_count + col

                @pl.when(inner < PT)
                def _():
                    value = low0_ref[pl.ds(place, tile), pl.ds(pl.multiple_of(jnp.minimum(inner, PT - 1) * tile, tile), tile)]
                    new_ref[a, c] = jnp.where(is_bf16, rounded(value), value)

                @pl.when((inner >= PT) & (row >= PT))
                def _():
                    lower = pl.multiple_of(jnp.clip(row - PT, 0, PT - 1) * tile, tile)
                    across = pl.multiple_of(jnp.clip(inner - PT, 0, PT - 1) * tile, tile)
                    value = low1_ref[pl.ds(lower, tile), pl.ds(across, tile)]
                    new_ref[a, c] = jnp.where(is_bf16, rounded(value), value)

                @pl.when(row < inner)
                def _():
                    new_ref[a, c] = jnp.zeros((tile, tile), jnp.float32)

    zero = jnp.zeros((tile, tile), jnp.float32)
    for a in range(tile_rows):
        for c in range(tile_cols):
            if c < first_col:
                panel_tile(a, c)
                write(a, c).start()
            elif a < c // groups or a < skip:
                new_ref[a, c] = zero
                write(a, c).start()
    raw_copy.wait()
    for b in range(skip, tile_rows):
        at = slice((b - skip) * tile, (b - skip + 1) * tile)
        lower = slice((b - skip) * tile, size)
        high = jnp.concatenate([high_ref[1 + g, at, :] for g in range(groups)], axis=0)
        rest = jnp.concatenate([rest_ref[1 + g, at, :] for g in range(groups)], axis=0)
        coarse = dot_bf16(high_ref[0, lower, :], high)
        more = dot_bf16(high_ref[0, lower, :], rest) + dot_bf16(rest_ref[0, lower, :], high)
        for a in range(b, tile_rows):
            for g in range(groups):
                c = b * groups + g
                if c < first_col:
                    continue
                here = (slice((a - b) * tile, (a - b + 1) * tile), span(g))
                is_bf16 = marks_ref[a, c] == 1
                value = raw_ref[a, c]
                exact = value - (coarse[here] + more[here])
                value = jnp.where(is_bf16, rounded(rounded(value) - coarse[here]), exact)
                new_ref[a, c] = jnp.where(a * row_count + row >= c * col_count + col, value, 0.0)
                write(a, c).start()
    for a in range(tile_rows):
        for c in range(tile_cols):
            write(a, c).wait()


def finish(marks, tiles, own, across, factors, row_count):
    low0, inv0, low1, inv1 = factors
    tile_rows, tile_cols, tile, _ = tiles.shape
    groups, col_count, rows, slots, height, _ = across.shape
    count = 2 * PT
    size = rows * tile
    hbm = pl.BlockSpec(memory_space=pltpu.HBM)
    dma = pltpu.SemaphoreType.DMA
    bf16 = lambda *shape: pltpu.VMEM(shape, jnp.bfloat16)
    f32 = lambda *shape: pltpu.VMEM(shape, jnp.float32)
    return pl.pallas_call(
        lambda *refs: finish_kernel(row_count, *refs),
        out_shape=jax.ShapeDtypeStruct(tiles.shape, jnp.float32),
        in_specs=[pl.BlockSpec(memory_space=pltpu.SMEM)] + [hbm] * 7,
        out_specs=hbm,
        scratch_shapes=[
            f32(1 + groups, col_count, rows, slots, height, tile),
            f32(*low0.shape),
            f32(*inv0.shape),
            f32(*low1.shape),
            f32(*inv1.shape),
            bf16(PT, 2 * tile, 6 * tile),
            bf16(2, PT // 2 - 1, 2 * tile, 6 * tile),
            bf16(PT * tile, PT * tile),
            bf16(PT * tile, PT * tile),
            bf16(1 + groups, size, count * tile),
            bf16(1 + groups, size, count * tile),
            f32(*tiles.shape),
            f32(*tiles.shape),
            dma((4,)),
            dma((1 + groups,)),
            dma(()),
            dma((tile_rows, tile_cols)),
        ],
        compiler_params=pltpu.CompilerParams(vmem_limit_bytes=60 * 1024 * 1024),
        name="finish",
    )(marks, tiles, own, across, low0, inv0, low1, inv1)


def on_device(matrix, flags):
    row_count = lax.axis_size("row")
    col_count = lax.axis_size("col")
    tile_rows = matrix.shape[0]
    tile_cols = matrix.shape[2]
    tile = matrix.shape[4]
    slots = 2 * PT // col_count
    tiles = matrix.reshape(tile_rows, tile_cols, tile, tile)
    marks = flags.reshape(tile_rows, tile_cols)

    head = tiles[:, :slots]
    head_marks = (marks[:, :slots] == 1)[:, :, None, None]
    stored = jnp.where(head_marks, lax.reduce_precision(head, 8, 7), head)
    tags = jnp.broadcast_to(head_marks.astype(jnp.float32), (tile_rows, slots, 8, tile))
    payload = jnp.concatenate([stored, tags], axis=2)

    own, across, *factors = exchange(payload, row_count, col_count)
    out = finish(marks, tiles, own, across, factors, row_count)
    return out.reshape(matrix.shape)


def solution(mesh):
    return jax.shard_map(
        on_device,
        mesh=mesh,
        in_specs=(P(None, "row", None, "col", None, None), P(None, "row", None, "col")),
        out_specs=P(None, "row", None, "col", None, None),
        check_vma=False,
    )
```

time: 176 us -> 151 us (0.86)
  Pallas kernels: 164 us -> 141 us
    pallas_call x3 -> x1, Pallas kernels: 41.1 us -> 17.4 us  [finish(): pl.pallas_call(lambda *refs: finish_kernel(row_count, *refs), out_shape=j...]
where the time goes in v2:
time: 151 us; the launch traced here: 150 us
  Pallas kernels  141 us (93%)
  local copies, waits for them, and re-layouts  8.21 us (5%)
    pallas_call x1, Pallas kernels, exchange(): pl.pallas_call(lambda *refs: exchange_kernel(dims, *refs), out_shape=(f32...  123 us
    pallas_call x1, Pallas kernels, finish(): pl.pallas_call(lambda *refs: finish_kernel(row_count, *refs), out_shape=j...  17.4 us
    unnamed x15, local copies, waits for them, and re-layouts  8.14 us

profile of v2, /device:TPU:9, one launch (start us, length us, event | category | flops | bytes accessed | tf_op | source)
XLA Modules:
  0.0 150.4 jit_solution(15156673068649493266)
XLA Ops:
  0.0 0.7 copy.6
  0.7 0.0 copy-start.6
  0.7 0.1 broadcast_in_dim.15
  0.8 1.2 reduce-precision_select_fusion
  2.0 123.3 %exchange.1 = (f32[4,4,2,136,128]{4,3,2,1,0:T(8,128)S(1)}, f32[2,4,4,2,136,128]{5,4,3,2,1,0:T(8,128)S(1)}, f32[1024,512]{1,0:T(8,128)S(1)}, f32[2,256,256]{2,1,0...) custom-call(f32[5,2,136,128]{3,2,1,0:T(8,128)S(1)} %pad_maximum_fusion.refs_0_), custom_call_target="tpu_custom_call" | custom-call | tf_op jit(solution)/shard_map/exchange/pallas_call | solution.py:368
  125.3 0.0 copy-start
  125.3 2.0 %copy-done = f32[2,4,4,2,136,128]{5,4,3,2,1,0:T(8,128)} copy-done((f32[2,4,4,2,136,128]{5,4,3,2,1,0:T(8,128)}, f32[2,4,4,2,136,128]{5,4,3,2,1,0:T(8,128)S(1)}, u32[]{:S(2)}) %copy-start) | copy-done | bytes 4456472
  127.3 0.0 copy-start.1
  127.3 1.4 copy-done.1
  128.7 0.0 copy-start.2
  128.8 1.4 copy-done.2
  130.1 0.0 copy-start.3
  130.1 1.0 copy-done.3
  131.2 0.0 copy-start.4
  131.2 0.8 copy-done.4
  132.0 0.0 copy-start.5
  132.0 0.8 copy-done.5
  132.8 0.0 copy-done.6
  132.8 17.4 %finish.1 = f32[5,10,128,128]{3,2,1,0:T(8,128)} custom-call(s32[5,10]{1,0:T(8,128)} %bitcast.10, f32[5,10,128,128]{3,2,1,0:T(8,128)} %bitcast.8, f32[4,4,2,136,128]{4,3,2,1,0:T(8,128)} %copy-done.1, f32[2,4,4,2,136,128]{5,4,3,2,1,0:T(8,128)} %copy-done, f32[1024,512]{1,0:T(8,128)} %copy-done.2, f32[2,256,256]{2,1,0:T(8,128)} %copy-done.4, ...), custom_call_target="tpu_custom_call" | custom-call | tf_op jit(solution)/shard_map/finish/pallas_call | solution.py:560
  (2 shorter events, 0.1 us)
Async XLA Ops:
  0.7 132.1 %copy-start.6 = (s32[5,1,10,1]{2,0,1,3:T(8,128)}, s32[5,1,10,1]{2,0,1,3:T(8,128)S(1)}, u32[]{:S(2)}) copy-start(s32[5,1,10,1]{2,0,1,3:T(8,128)S(1)} %copy.6) | copy-start | bytes 604
  125.3 2.0 %copy-start = (f32[2,4,4,2,136,128]{5,4,3,2,1,0:T(8,128)}, f32[2,4,4,2,136,128]{5,4,3,2,1,0:T(8,128)S(1)}, u32[]{:S(2)}) copy-start(f32[2,4,4,2,136,128]{5,4,3,2,1,0:T(8,128)S(1)} %get-tuple-element.12.refs_3_) | copy-start | bytes 13369348
  127.3 1.4 copy-start.1
  128.7 1.4 copy-start.2
  130.1 1.0 copy-start.3
  131.2 0.8 copy-start.4
  132.0 0.8 copy-start.5

commit v3 on v2

--- a/solution.py
+++ b/solution.py
@@ -107,10 +107,10 @@
     low_ref[...] += upper_ref[...].T
 
 
-def exchange_kernel(dims, p_ref, own_ref, across_ref, low0_ref, inv0_ref, low1_ref, inv1_ref,
+def exchange_kernel(dims, p_ref, panel_ref, through_ref, low0_ref, inv0_ref, low1_ref, inv1_ref,
                     grid_ref, relay_ref, work_ref, up_ref,
                     line_send, line_recv, spread_send, grid_recv, own_send, own_recv,
-                    column_send, across_recv, cross_send, result_send, result_recv, local_sem):
+                    chain_send, chain_recv, side_send, extra_send, across_recv, cross_send, result_send, result_recv, local_sem):
     rows, cols, slots, skip, tile = dims
     count = 2 * PT
     groups = rows // cols
@@ -123,6 +123,8 @@
     works = (row + col) % 2 == 1
     partner = wide * 2 + 1 - core
     bulk = p_ref.at[skip:]
+    own_ref = panel_ref.at[0]
+    across_ref = panel_ref.at[1:]
 
     def copy(src, dst, send, recv, to_row, to_col):
         return pltpu.make_async_remote_copy(
@@ -168,39 +170,103 @@
                                  line_recv.at[k, c, s], row, partner).wait_recv()
                         targets(relay_ref.at[k, c, s])
 
-    def own_copies(act):
-        for k in range(1, cols):
-            act(copy(bulk, own_ref.at[col], own_send.at[k], own_recv.at[col], row, (col + k) % cols))
-
-    def column_copies(act):
-        for k in range(lines):
-            @pl.when(jnp.logical_not((k == along) & (col == row % cols)))
-            def _():
-                act(copy(bulk, across_ref.at[row // cols, col], column_send.at[k],
-                         across_recv.at[row // cols, col], 2 * k + side, row % cols))
-
-    def cross(act, wait):
-        near = jnp.clip((along - wide + cols // 4) // (cols // 2), 0, groups - 1)
-        for k in range(cols):
-            from_col = (wide + k // 2) % (cols // 2) * 2 + (core + k) % 2
-            for h in range(groups):
-                g = (near + h) % groups
-                mine = (g * cols + col == row) & (from_col == col)
-
-                def forward(src):
-                    return copy(src, across_ref.at[g, from_col], cross_send.at[g, from_col],
-                                across_recv.at[g, from_col], 2 * along + 1 - side, col)
-
-                @pl.when(mine)
-                def _():
-                    act(forward(bulk))
-
-                @pl.when(jnp.logical_not(mine))
-                def _():
-                    move = forward(across_ref.at[g, from_col])
-                    if wait:
-                        move.wait_recv()
-                    act(move)
+    wides = cols // 2
+    group = row // cols
+    direct_here = along % wides == wide
+
+    def own_copies(act, first, last):
+        for k in range(first, last):
+            to_col = (wide + (k + 1) // 2) % wides * 2 + (core + 1 + k) % 2
+            act(copy(bulk, own_ref.at[col], own_send.at[k], own_recv.at[col], row, to_col))
+
+    def extra_copy():
+        return copy(bulk, across_ref.at[group, col], extra_send.at[0], across_recv.at[group, col], row, partner)
+
+    def chain_step(d, act, wait, onward, plane):
+        for up in (0, 1) if d else (0,):
+            k = along + d if up else along - d
+            g = (2 * k + side) // cols
+            direct = k % wides == wide
+            for c in range(2):
+                from_col = wide * 2 + c
+
+                def send(src, dst):
+                    if onward:
+                        if not (d and up):
+                            @pl.when(along < lines - 1)
+                            def _():
+                                act(copy(src, dst, chain_send.at[0, k, c], chain_recv.at[k, c], row + 2, col))
+
+                        if not d or up:
+                            @pl.when(along > 0)
+                            def _():
+                                act(copy(src, dst, chain_send.at[1, k, c], chain_recv.at[k, c], row - 2, col))
+
+                def send_plane(src):
+                    if plane:
+                        @pl.when(direct)
+                        def _():
+                            act(copy(src, across_ref.at[g, from_col], cross_send.at[g, from_col],
+                                     across_recv.at[g, from_col], 2 * along + 1 - side, col))
+
+                        @pl.when(jnp.logical_not(direct))
+                        def _():
+                            act(copy(src, across_ref.at[g, from_col], side_send.at[k, c],
+                                     across_recv.at[g, from_col], row, (2 * k + side) % cols))
+
+                def send_all(src):
+                    @pl.when(direct)
+                    def _():
+                        send(src, across_ref.at[g, from_col])
+
+                    @pl.when(jnp.logical_not(direct))
+                    def _():
+                        send(src, through_ref.at[k, c])
+                    send_plane(src)
+
+                if not d:
+                    @pl.when(core == c)
+                    def _():
+                        send_all(bulk)
+
+                    @pl.when(core != c)
+                    def _():
+                        if wait and onward:
+                            copy(bulk, own_ref.at[from_col], own_send.at[0], own_recv.at[from_col], row, partner).wait_recv()
+                        send_all(own_ref.at[from_col])
+                else:
+                    @pl.when((k >= 0) & (k < lines) & direct)
+                    def _():
+                        here = across_ref.at[g, from_col]
+                        if wait:
+                            copy(bulk, here, own_send.at[0], chain_recv.at[k, c], row, partner).wait_recv()
+                        send(here, here)
+                        send_plane(here)
+
+                    @pl.when((k >= 0) & (k < lines) & jnp.logical_not(direct))
+                    def _():
+                        here = through_ref.at[k, c]
+                        if wait:
+                            copy(bulk, here, own_send.at[0], chain_recv.at[k, c], row, partner).wait_recv()
+                        send(here, here)
+                        send_plane(here)
+
+    def side_step(d, act, wait):
+        for up in (0, 1) if d else (0,):
+            k = along + d if up else along - d
+            g = (2 * k + side) // cols
+            for w in range(1, wides):
+                for c in range(2):
+                    from_col = (wide + w) % wides * 2 + c
+
+                    @pl.when((k >= 0) & (k < lines) & (k % wides == wide))
+                    def _():
+                        here = across_ref.at[g, from_col]
+                        move = copy(here, here, cross_send.at[g, from_col], across_recv.at[g, from_col],
+                                    2 * along + 1 - side, col)
+                        if wait:
+                            move.wait_recv()
+                        act(move)
 
     def wait_grid(first, last):
         for i in range(first, last):
@@ -208,9 +274,9 @@
                 at = (i, j % cols, j // cols)
                 copy(p_ref.at[0, 0], grid_ref.at[at], line_send.at[0, 0], grid_recv.at[at], row, partner).wait_recv()
 
-    def wait_own():
-        for k in range(1, cols):
-            c = (col + k) % cols
+    def wait_own(first, last):
+        for k in range(first, last):
+            c = (wide + (k + 1) // 2) % wides * 2 + (core + 1 + k) % 2
             copy(bulk, own_ref.at[c], own_send.at[k], own_recv.at[c], row, partner).wait_recv()
 
     results = (low0_ref, inv0_ref, low1_ref, inv1_ref)
@@ -234,17 +300,26 @@
     @pl.when(relays)
     def _():
         spread_copies(0, PT, start, True)
+        chain_step(0, start, True, True, True)
         spread_copies(PT, count, start, True)
-        column_copies(start)
-        own_copies(start)
-        cross(start, True)
+        own_copies(start, 0, 1)
+        for d in range(1, lines):
+            chain_step(d, start, True, True, True)
+            side_step(d - 1, start, True)
+            if d == 1:
+                own_copies(start, 1, cols - 1)
+        side_step(lines - 1, start, True)
 
     @pl.when(works)
     def _():
+        own_copies(start, 0, 1)
+
+        @pl.when(direct_here)
+        def _():
+            extra_copy().start()
         wait_grid(0, PT)
-        column_copies(start)
-        own_copies(start)
         factor_first(cols, tile, grid_ref, low0_ref, inv0_ref, work_ref, up_ref)
+        own_copies(start, 1, cols - 1)
         wait_grid(PT, count)
         factor_rest(cols, tile, grid_ref, low0_ref, inv0_ref)
         factor_second(cols, tile, grid_ref, low0_ref, low1_ref, inv1_ref, work_ref, up_ref,
@@ -256,19 +331,29 @@
         for g in range(groups):
             for c in range(cols):
                 copy(bulk, across_ref.at[g, c], own_send.at[0], across_recv.at[g, c], row, partner).wait_recv()
+        wait_own(0, 1)
+
+        @pl.when(direct_here)
+        def _():
+            extra_copy().wait_send()
 
     line_copies(done)
 
     @pl.when(relays)
     def _():
         spread_copies(0, count, done, False)
-        cross(done, False)
+        for d in range(lines):
+            chain_step(d, done, False, True, True)
+            side_step(d, done, False)
+
+        @pl.when(direct_here)
+        def _():
+            copy(bulk, across_ref.at[group, partner], own_send.at[0], across_recv.at[group, partner], row, partner).wait_recv()
         for k in range(4):
             result_copy(k).wait_recv()
 
-    column_copies(done)
-    own_copies(done)
-    wait_own()
+    own_copies(done, 0, cols - 1)
+    wait_own(1, cols - 1)
     keep.wait()
 
     @pl.when(source)
@@ -368,8 +453,8 @@
     return pl.pallas_call(
         lambda *refs: exchange_kernel(dims, *refs),
         out_shape=(
-            f32(cols, *part),
-            f32(groups, cols, *part),
+            f32(1 + groups, cols, *part),
+            f32(rows // 2, 2, *part),
             f32(count * tile, PT * tile),
             f32(PT // 2, 2 * tile, 2 * tile),
             f32(PT * tile, PT * tile),
@@ -388,7 +473,10 @@
             dma((count, cols, slots)),
             dma((cols,)),
             dma((cols,)),
-            dma((rows // 2,)),
+            dma((2, rows // 2, 2)),
+            dma((rows // 2, 2)),
+            dma((rows // 2, 2)),
+            dma((1,)),
             dma((groups, cols)),
             dma((groups, cols)),
             dma((4,)),
@@ -400,10 +488,10 @@
     )(payload)
 
 
-def finish_kernel(row_count, marks_ref, tiles_ref, own_ref, across_ref, low0_hbm, inv0_hbm, low1_hbm, inv1_hbm,
-                  out_ref, panel_ref, low0_ref, inv0_ref, low1_ref, inv1_ref, inv_ref, under_ref, cross_h, cross_l,
-                  high_ref, rest_ref, raw_ref, new_ref, factor_sem, panel_sem, raw_sem, new_sem):
-    groups, col_count, rows, slots, height, tile = across_ref.shape
+def finish_kernel(row_count, marks_ref, tiles_ref, panel_ref, low0_ref, inv0_ref, low1_ref, inv1_ref,
+                  out_ref, inv_ref, under_ref, cross_h, cross_l, high_ref, rest_ref, new_ref, new_sem):
+    groups, col_count, rows, slots, height, tile = panel_ref.shape
+    groups -= 1
     tile_rows, tile_cols = tiles_ref.shape[:2]
     count = 2 * PT
     width = PT * tile
@@ -414,19 +502,6 @@
     col = lax.axis_index("col")
     span = span_of(tile)
 
-    factor_copies = [
-        pltpu.make_async_copy(src, dst, factor_sem.at[k])
-        for k, (src, dst) in enumerate(
-            ((inv0_hbm, inv0_ref), (low0_hbm, low0_ref), (inv1_hbm, inv1_ref), (low1_hbm, low1_ref))
-        )
-    ]
-    panel_copies = [pltpu.make_async_copy(own_ref, panel_ref.at[0], panel_sem.at[0])] + [
-        pltpu.make_async_copy(across_ref.at[g], panel_ref.at[1 + g], panel_sem.at[1 + g]) for g in range(groups)
-    ]
-    raw_copy = pltpu.make_async_copy(tiles_ref, raw_ref, raw_sem)
-    for move in (factor_copies[0], panel_copies[0], *factor_copies[1:], *panel_copies[1:], raw_copy):
-        move.start()
-
     def stacked(value):
         high, rest = split(value)
         return jnp.concatenate([high, high, rest], axis=1)
@@ -435,8 +510,6 @@
         high, rest = split(value)
         return dot_bf16(jnp.concatenate([high, rest, high], axis=1), weights)
 
-    for move in factor_copies:
-        move.wait()
     for k in range(PT // 2):
         inv_ref[k] = stacked(inv0_ref[k])
         inv_ref[PT // 2 + k] = stacked(inv1_ref[k])
@@ -446,8 +519,6 @@
     cross_h[...], cross_l[...] = split(low0_ref[span(PT, count), :])
 
     def solve(group, carry):
-        pltpu.make_async_copy(own_ref, panel_ref.at[group], panel_sem.at[group]).wait()
-
         def column(t):
             return panel_ref[group, t % col_count, :, t // col_count, :tile, :].reshape(size, tile)
 
@@ -522,7 +593,6 @@
             elif a < c // groups or a < skip:
                 new_ref[a, c] = zero
                 write(a, c).start()
-    raw_copy.wait()
     for b in range(skip, tile_rows):
         at = slice((b - skip) * tile, (b - skip + 1) * tile)
         lower = slice((b - skip) * tile, size)
@@ -537,7 +607,7 @@
                     continue
                 here = (slice((a - b) * tile, (a - b + 1) * tile), span(g))
                 is_bf16 = marks_ref[a, c] == 1
-                value = raw_ref[a, c]
+                value = tiles_ref[a, c]
                 exact = value - (coarse[here] + more[here])
                 value = jnp.where(is_bf16, rounded(rounded(value) - coarse[here]), exact)
                 new_ref[a, c] = jnp.where(a * row_count + row >= c * col_count + col, value, 0.0)
@@ -547,27 +617,26 @@
             write(a, c).wait()
 
 
-def finish(marks, tiles, own, across, factors, row_count):
+def finish(marks, tiles, panels, factors, row_count):
     low0, inv0, low1, inv1 = factors
     tile_rows, tile_cols, tile, _ = tiles.shape
-    groups, col_count, rows, slots, height, _ = across.shape
+    groups, col_count, rows, slots, height, _ = panels.shape
+    groups -= 1
     count = 2 * PT
     size = rows * tile
     hbm = pl.BlockSpec(memory_space=pltpu.HBM)
+    vmem = pl.BlockSpec(memory_space=pltpu.VMEM)
     dma = pltpu.SemaphoreType.DMA
     bf16 = lambda *shape: pltpu.VMEM(shape, jnp.bfloat16)
     f32 = lambda *shape: pltpu.VMEM(shape, jnp.float32)
+    held = 2 * tiles.size + panels.size + low0.size + inv0.size + low1.size + inv1.size
+    held += (1 + groups) * size * count * tile + 2 * PT * tile * PT * tile
     return pl.pallas_call(
         lambda *refs: finish_kernel(row_count, *refs),
         out_shape=jax.ShapeDtypeStruct(tiles.shape, jnp.float32),
-        in_specs=[pl.BlockSpec(memory_space=pltpu.SMEM)] + [hbm] * 7,
+        in_specs=[pl.BlockSpec(memory_space=pltpu.SMEM)] + [vmem] * 6,
         out_specs=hbm,
         scratch_shapes=[
-            f32(1 + groups, col_count, rows, slots, height, tile),
-            f32(*low0.shape),
-            f32(*inv0.shape),
-            f32(*low1.shape),
-            f32(*inv1.shape),
             bf16(PT, 2 * tile, 6 * tile),
             bf16(2, PT // 2 - 1, 2 * tile, 6 * tile),
             bf16(PT * tile, PT * tile),
@@ -575,15 +644,11 @@
             bf16(1 + groups, size, count * tile),
             bf16(1 + groups, size, count * tile),
             f32(*tiles.shape),
-            f32(*tiles.shape),
-            dma((4,)),
-            dma((1 + groups,)),
-            dma(()),
             dma((tile_rows, tile_cols)),
         ],
-        compiler_params=pltpu.CompilerParams(vmem_limit_bytes=60 * 1024 * 1024),
+        compiler_params=pltpu.CompilerParams(vmem_limit_bytes=4 * held + 12 * 1024 * 1024),
         name="finish",
-    )(marks, tiles, own, across, low0, inv0, low1, inv1)
+    )(marks, tiles, panels, low0, inv0, low1, inv1)
 
 
 def on_device(matrix, flags):
@@ -602,8 +667,8 @@
     tags = jnp.broadcast_to(head_marks.astype(jnp.float32), (tile_rows, slots, 8, tile))
     payload = jnp.concatenate([stored, tags], axis=2)
 
-    own, across, *factors = exchange(payload, row_count, col_count)
-    out = finish(marks, tiles, own, across, factors, row_count)
+    panels, _, *factors = exchange(payload, row_count, col_count)
+    out = finish(marks, tiles, panels, factors, row_count)
     return out.reshape(matrix.shape)
 
 

time: 151 us -> 107 us (0.71)
  the two profiles are of different devices: /device:TPU:9 before, /device:TPU:5 now
where the time goes in v3:
time: 107 us
  Pallas kernels  104 us (97%)
  other arithmetic  1.36 us (1%)
    pallas_call x1, Pallas kernels, exchange(): pl.pallas_call(lambda *refs: exchange_kernel(dims, *refs), out_shape=(f32...  90.2 us
    pallas_call x1, Pallas kernels, finish(): pl.pallas_call(lambda *refs: finish_kernel(row_count, *refs), out_shape=j...  13.9 us

profile of v3, /device:TPU:5, one launch (start us, length us, event | category | flops | bytes accessed | tf_op | source)
XLA Modules:
  0.0 106.5 jit_solution(6424780283483531867)
XLA Ops:
  0.0 0.0 copy-start
  0.0 0.8 copy.6
  0.8 0.1 broadcast_in_dim.15
  0.9 1.3 %reduce-precision_select_fusion = f32[5,2,128,128]{3,2,1,0:T(8,128)S(1)} fusion(f32[5,10,128,128]{3,2,1,0:T(8,128)} %bitcast.7, pred[5,2]{1,0:T(8,128)(4,1)S(1)} %get-tuple-element.16), kind=kLoop, calls=%fused_computation | loop fusion | flops 327680 | bytes 1310730 | tf_op jit(solution)/shard_map/jit(_where)/select_n | solution.py:666
  2.3 90.2 %exchange.1 = (f32[3,4,4,2,136,128]{5,4,3,2,1,0:T(8,128)S(1)}, f32[4,2,4,2,136,128]{5,4,3,2,1,0:T(8,128)}, f32[1024,512]{1,0:T(8,128)S(1)}, f32[2,256,256]{2,1,0...) custom-call(f32[5,2,136,128]{3,2,1,0:T(8,128)S(1)} %pad_maximum_fusion.refs_0_), custom_call_target="tpu_custom_call" | custom-call | tf_op jit(solution)/shard_map/exchange/pallas_call | solution.py:453
  92.4 0.0 copy-done
  92.5 13.9 %finish.1 = f32[5,10,128,128]{3,2,1,0:T(8,128)} custom-call(s32[5,10]{1,0:T(8,128)S(1)} %bitcast.10, f32[5,10,128,128]{3,2,1,0:T(8,128)S(1)} %bitcast.8, f32[3,4,4,2,136,128]{5,4,3,2,1,0:T(8,128)S(1)} %get-tuple-element.10.refs_2_, f32[1024,512]{1,0:T(8,128)S(1)} %get-tuple-element.11.refs_3_, f32[2,256,256]{2,1,0:T(8,128)S(1)} %get-tuple-element.12.refs_4_, ...), custom_call_target="tpu_custom_call" | custom-call | tf_op jit(solution)/shard_map/finish/pallas_call | solution.py:634
  (2 shorter events, 0.1 us)
Async XLA Ops:
  0.0 92.4 %copy-start = (f32[5,1,10,1,128,128]{5,4,3,2,1,0:T(8,128)S(1)}, f32[5,1,10,1,128,128]{5,4,3,2,1,0:T(8,128)}, u32[]{:S(2)}) copy-start(f32[5,1,10,1,128,128]{5,4,3,2,1,0:T(8,128)} %param.2) | copy-start | bytes 9830404

commit v4 on v3

--- a/solution.py
+++ b/solution.py
@@ -179,11 +179,16 @@
             to_col = (wide + (k + 1) // 2) % wides * 2 + (core + 1 + k) % 2
             act(copy(bulk, own_ref.at[col], own_send.at[k], own_recv.at[col], row, to_col))
 
-    def extra_copy():
-        return copy(bulk, across_ref.at[group, col], extra_send.at[0], across_recv.at[group, col], row, partner)
+    middle = bulk.shape[0] // 2
+    halves = (slice(0, middle), slice(middle, bulk.shape[0]))
+
+    def extra_copy(h):
+        return copy(bulk.at[halves[h]], across_ref.at[group, col, halves[h]], extra_send.at[h],
+                    across_recv.at[group, col, h], row, partner)
 
     def chain_step(d, act, wait, onward, plane):
-        for up in (0, 1) if d else (0,):
+        for up, h in ((u, h) for u in ((0, 1) if d else (0,)) for h in range(2)):
+            part = halves[h]
             k = along + d if up else along - d
             g = (2 * k + side) // cols
             direct = k % wides == wide
@@ -195,64 +200,65 @@
                         if not (d and up):
                             @pl.when(along < lines - 1)
                             def _():
-                                act(copy(src, dst, chain_send.at[0, k, c], chain_recv.at[k, c], row + 2, col))
+                                act(copy(src, dst, chain_send.at[0, k, c, h], chain_recv.at[k, c, h], row + 2, col))
 
                         if not d or up:
                             @pl.when(along > 0)
                             def _():
-                                act(copy(src, dst, chain_send.at[1, k, c], chain_recv.at[k, c], row - 2, col))
+                                act(copy(src, dst, chain_send.at[1, k, c, h], chain_recv.at[k, c, h], row - 2, col))
 
                 def send_plane(src):
                     if plane:
                         @pl.when(direct)
                         def _():
-                            act(copy(src, across_ref.at[g, from_col], cross_send.at[g, from_col],
-                                     across_recv.at[g, from_col], 2 * along + 1 - side, col))
+                            act(copy(src, across_ref.at[g, from_col, part], cross_send.at[g, from_col, h],
+                                     across_recv.at[g, from_col, h], 2 * along + 1 - side, col))
 
                         @pl.when(jnp.logical_not(direct))
                         def _():
-                            act(copy(src, across_ref.at[g, from_col], side_send.at[k, c],
-                                     across_recv.at[g, from_col], row, (2 * k + side) % cols))
+                            act(copy(src, across_ref.at[g, from_col, part], side_send.at[k, c, h],
+                                     across_recv.at[g, from_col, h], row, (2 * k + side) % cols))
 
                 def send_all(src):
                     @pl.when(direct)
                     def _():
-                        send(src, across_ref.at[g, from_col])
+                        send(src, across_ref.at[g, from_col, part])
 
                     @pl.when(jnp.logical_not(direct))
                     def _():
-                        send(src, through_ref.at[k, c])
+                        send(src, through_ref.at[k, c, part])
                     send_plane(src)
 
                 if not d:
                     @pl.when(core == c)
                     def _():
-                        send_all(bulk)
+                        send_all(bulk.at[part])
 
                     @pl.when(core != c)
                     def _():
-                        if wait and onward:
+                        if wait and onward and h == 0:
                             copy(bulk, own_ref.at[from_col], own_send.at[0], own_recv.at[from_col], row, partner).wait_recv()
-                        send_all(own_ref.at[from_col])
+                        send_all(own_ref.at[from_col, part])
                 else:
                     @pl.when((k >= 0) & (k < lines) & direct)
                     def _():
-                        here = across_ref.at[g, from_col]
+                        here = across_ref.at[g, from_col, part]
                         if wait:
-                            copy(bulk, here, own_send.at[0], chain_recv.at[k, c], row, partner).wait_recv()
+                            copy(bulk.at[part], here, own_send.at[0], chain_recv.at[k, c, h], row, partner).wait_recv()
                         send(here, here)
                         send_plane(here)
 
                     @pl.when((k >= 0) & (k < lines) & jnp.logical_not(direct))
                     def _():
-                        here = through_ref.at[k, c]
+                        here = through_ref.at[k, c, part]
                         if wait:
-                            copy(bulk, here, own_send.at[0], chain_recv.at[k, c], row, partner).wait_recv()
+                            copy(bulk.at[part], here, own_send.at[0], chain_recv.at[k, c, h], row, partner).wait_recv()
                         send(here, here)
                         send_plane(here)
 
     def side_step(d, act, wait):
-        for up in (0, 1) if d else (0,):
+        for up, h in ((u, h) for u in ((0, 1) if d else (0,)) for h in range(2)):
+            part = halves[h]
             k = along + d if up else along - d
             g = (2 * k + side) // cols
             for w in range(1, wides):
@@ -261,8 +267,8 @@
 
                     @pl.when((k >= 0) & (k < lines) & (k % wides == wide))
                     def _():
-                        here = across_ref.at[g, from_col]
-                        move = copy(here, here, cross_send.at[g, from_col], across_recv.at[g, from_col],
+                        here = across_ref.at[g, from_col, part]
+                        move = copy(here, here, cross_send.at[g, from_col, h], across_recv.at[g, from_col, h],
                                     2 * along + 1 - side, col)
                         if wait:
                             move.wait_recv()
@@ -316,7 +322,8 @@
 
         @pl.when(direct_here)
         def _():
-            extra_copy().start()
+            extra_copy(0).start()
+            extra_copy(1).start()
         wait_grid(0, PT)
         factor_first(cols, tile, grid_ref, low0_ref, inv0_ref, work_ref, up_ref)
         own_copies(start, 1, cols - 1)
@@ -330,12 +337,15 @@
             result_copy(k).wait_send()
         for g in range(groups):
             for c in range(cols):
-                copy(bulk, across_ref.at[g, c], own_send.at[0], across_recv.at[g, c], row, partner).wait_recv()
+                for h in range(2):
+                    copy(bulk.at[halves[h]], across_ref.at[g, c, halves[h]], own_send.at[0], across_recv.at[g, c, h],
+                         row, partner).wait_recv()
         wait_own(0, 1)
 
         @pl.when(direct_here)
         def _():
-            extra_copy().wait_send()
+            extra_copy(0).wait_send()
+            extra_copy(1).wait_send()
 
     line_copies(done)
 
@@ -348,7 +358,9 @@
 
         @pl.when(direct_here)
         def _():
-            copy(bulk, across_ref.at[group, partner], own_send.at[0], across_recv.at[group, partner], row, partner).wait_recv()
+            for h in range(2):
+                copy(bulk.at[halves[h]], across_ref.at[group, partner, halves[h]], own_send.at[0],
+                     across_recv.at[group, partner, h], row, partner).wait_recv()
         for k in range(4):
             result_copy(k).wait_recv()
 
@@ -473,12 +485,12 @@
             dma((count, cols, slots)),
             dma((cols,)),
             dma((cols,)),
-            dma((2, rows // 2, 2)),
-            dma((rows // 2, 2)),
-            dma((rows // 2, 2)),
-            dma((1,)),
-            dma((groups, cols)),
-            dma((groups, cols)),
+            dma((2, rows // 2, 2, 2)),
+            dma((rows // 2, 2, 2)),
+            dma((rows // 2, 2, 2)),
+            dma((2,)),
+            dma((groups, cols, 2)),
+            dma((groups, cols, 2)),
             dma((4,)),
             dma((4,)),
             dma((2,)),
@@ -501,6 +513,15 @@
     row = lax.axis_index("row")
     col = lax.axis_index("col")
     span = span_of(tile)
+
+    def write(a, c):
+        return pltpu.make_async_copy(new_ref.at[a, c], out_ref.at[a, c], new_sem.at[a, c])
+
+    for a in range(tile_rows):
+        for c in range(first_col, tile_cols):
+            if a < c // groups or a < skip:
+                new_ref[a, c] = jnp.zeros((tile, tile), jnp.float32)
+                write(a, c).start()
 
     def stacked(value):
         high, rest = split(value)
@@ -552,9 +573,6 @@
     def rounded(value):
         return value.astype(jnp.bfloat16).astype(jnp.float32)
 
-    def write(a, c):
-        return pltpu.make_async_copy(new_ref.at[a, c], out_ref.at[a, c], new_sem.at[a, c])
-
     def panel_tile(a, c):
         base = pl.multiple_of((c * col_count + col) * tile, tile)
         is_bf16 = marks_ref[a, c] == 1
@@ -584,14 +602,10 @@
                 def _():
                     new_ref[a, c] = jnp.zeros((tile, tile), jnp.float32)
 
-    zero = jnp.zeros((tile, tile), jnp.float32)
     for a in range(tile_rows):
         for c in range(tile_cols):
             if c < first_col:
                 panel_tile(a, c)
-                write(a, c).start()
-            elif a < c // groups or a < skip:
-                new_ref[a, c] = zero
                 write(a, c).start()
     for b in range(skip, tile_rows):
         at = slice((b - skip) * tile, (b - skip + 1) * tile)

time: 107 us -> 104 us (0.972)
  Pallas kernels: 104 us -> 102 us
    pallas_call x1, Pallas kernels: 90.2 us -> 87.6 us  [exchange(): pl.pallas_call(lambda *refs: exchange_kernel(dims, *refs), out_shape=(f32...]
where the time goes in v4:
time: 104 us
  Pallas kernels  102 us (98%)
  other arithmetic  1.36 us (1%)
    pallas_call x1, Pallas kernels, exchange(): pl.pallas_call(lambda *refs: exchange_kernel(dims, *refs), out_shape=(f32...  87.6 us
    pallas_call x1, Pallas kernels, finish(): pl.pallas_call(lambda *refs: finish_kernel(row_count, *refs), out_shape=j...  13.9 us

profile of v4, /device:TPU:5, one launch (start us, length us, event | category | flops | bytes accessed | tf_op | source)
XLA Modules:
  0.0 104.0 jit_solution(322188297468626363)
XLA Ops:
  0.0 0.0 copy-start
  0.0 0.8 copy.6
  0.8 0.1 broadcast_in_dim.15
  0.9 1.3 %reduce-precision_select_fusion = f32[5,2,128,128]{3,2,1,0:T(8,128)S(1)} fusion(f32[5,10,128,128]{3,2,1,0:T(8,128)} %bitcast.7, pred[5,2]{1,0:T(8,128)(4,1)S(1)} %get-tuple-element.16), kind=kLoop, calls=%fused_computation | loop fusion | flops 327680 | bytes 1310730 | tf_op jit(solution)/shard_map/jit(_where)/select_n | solution.py:680
  2.3 87.6 %exchange.1 = (f32[3,4,4,2,136,128]{5,4,3,2,1,0:T(8,128)S(1)}, f32[4,2,4,2,136,128]{5,4,3,2,1,0:T(8,128)}, f32[1024,512]{1,0:T(8,128)S(1)}, f32[2,256,256]{2,1,0...) custom-call(f32[5,2,136,128]{3,2,1,0:T(8,128)S(1)} %pad_maximum_fusion.refs_0_), custom_call_target="tpu_custom_call" | custom-call | tf_op jit(solution)/shard_map/exchange/pallas_call | solution.py:465
  89.9 0.0 copy-done
  89.9 13.9 %finish.1 = f32[5,10,128,128]{3,2,1,0:T(8,128)} custom-call(s32[5,10]{1,0:T(8,128)S(1)} %bitcast.10, f32[5,10,128,128]{3,2,1,0:T(8,128)S(1)} %bitcast.8, f32[3,4,4,2,136,128]{5,4,3,2,1,0:T(8,128)S(1)} %get-tuple-element.10.refs_2_, f32[1024,512]{1,0:T(8,128)S(1)} %get-tuple-element.11.refs_3_, f32[2,256,256]{2,1,0:T(8,128)S(1)} %get-tuple-element.12.refs_4_, ...), custom_call_target="tpu_custom_call" | custom-call | tf_op jit(solution)/shard_map/finish/pallas_call | solution.py:648
  (2 shorter events, 0.1 us)
Async XLA Ops:
  0.0 89.9 %copy-start = (f32[5,1,10,1,128,128]{5,4,3,2,1,0:T(8,128)S(1)}, f32[5,1,10,1,128,128]{5,4,3,2,1,0:T(8,128)}, u32[]{:S(2)}) copy-start(f32[5,1,10,1,128,128]{5,4,3,2,1,0:T(8,128)} %param.2) | copy-start | bytes 9830404
